TPU v7x, 256 devices: a whole 4x4x8 slice. The times are simulated.
256 devices in a mesh: down: 32 (over y, z_lo, core), cross: 8 (over x, z_hi).
Axes of the slice: x: 4, y: 4, z: 8 (z_hi: 2, z_lo: 4; z = z_hi * 4 + z_lo), core: 2. Of those that a mesh axis runs over, the one named last changes fastest.
Arguments:
- position: float32 [3, 16384, 128], P(None, ('down', 'cross')), may hold values from 0.5 to 4.5, as said below
- velocity: float32 [3, 16384, 128], P(None, ('down', 'cross')), may hold values from -6 to 6
- affine: float32 [9, 16384, 128], P(None, ('down', 'cross')), may hold values from -3 to 3
- deform: float32 [9, 16384, 128], P(None, ('down', 'cross')), may hold values from -0.1 to 1.2, as said below
- particle_mass: float32 [16384, 128], P(('down', 'cross')), may hold values from 0.5 to 2
- block_count: int32 [16384], P(('down', 'cross')), may hold values from 0 to 128, as said below
- block_brick: int32 [16384], P(('down', 'cross')), may hold values from 0 to 2047
- boundary_mask: int32 [512, 128, 128], P('down', 'cross'), may hold values 0 or 1
- leaving_block: int32 [16384], P(('down', 'cross')), may hold values from 0 to 63, as said below
- leaving_dest: int32 [16384], P(('down', 'cross')), may hold values from 0 to 8, as said below
Outputs:
- new_state: float32 [24, 16384, 128], P(None, ('down', 'cross'))
- arrivals: float32 [25, 16384, 128], P(None, ('down', 'cross'))
Inputs may be any that keep to these rules, and one draw needn't show every extreme that they name: `position`: component 0 lies in 0.5 to 2 + 0.5, component 1 in 0.5 to 2 + 0.5, component 2 in 0.5 to 4 + 0.5. `deform`: rows 0, 4 and 8 (the diagonal) lie in 0.8 to 1.2, the other rows in -0.1 to 0.1. `block_count`: the first block of every device holds 128 live particles. `leaving_block`: the entries of one device name distinct blocks. `leaving_dest`: id 4 marks an unused entry; no device names one id more than 8 times; every device names id 7 exactly 8 times; in every draw each neighbour of some device names the id that points to that device 8 times.
All inputs are finite; a program needn't handle non-finite values. No bound on the sum of `boundary_mask` on one device may be relied on, other than what follows from the above.
Results may differ from a plain program's by a relative error of at most 0.0003.
Values sent between devices are 32-bit elements; how exact they have to be, the bound alone decides.
A program may use at most 64 MiB of HBM per device.

v0:
```python
import jax
import jax.numpy as jnp
from jax import lax
from jax.sharding import PartitionSpec as P

GX = 16
GY = 16
GZ = 128
SLOTS = 128
BX = 2
BY = 2
BZ = 4
MIG = 8
NBX = 8
NBY = 8


time_step = 0.05
shear_modulus = 8.0
lame_first = 12.0
stress_factor = 0.2
gravity = (2.0, 0.0, -9.0)
mass_floor = 1.0
highest = lax.Precision.HIGHEST
move_list = ((-1, -1), (-1, 0), (-1, 1), (0, -1), (0, 1), (1, -1), (1, 0), (1, 1))


def passed_along(value, axis, steps):
    count = lax.axis_size(axis)
    leading, last = (max(0, -steps), min(count, count - steps))
    return lax.ppermute(value, axis, [(source, source + steps) for source in range(leading, last)])


def spline(distance):
    magnitude = jnp.abs(distance)
    inner_part = 0.75 - magnitude * magnitude
    outer_part = 0.5 * jnp.square(jnp.maximum(1.5 - magnitude, 0.0))
    return jnp.where(magnitude < 0.5, inner_part, outer_part)


def node_offsets():
    along_x = jnp.arange(2 * BX, dtype=jnp.float32)
    along_y = jnp.arange(2 * BY, dtype=jnp.float32)
    along_z = jnp.arange(2 * BZ, dtype=jnp.float32)
    node_shape = (2 * BX, 2 * BY, 2, BZ)
    halves = jnp.arange(2, dtype=jnp.float32)
    cells = jnp.arange(BZ, dtype=jnp.float32)
    height = halves[:, None] * BZ + cells[None, :]
    coords = jnp.stack(
        [
            jnp.broadcast_to(along_x[:, None, None, None], node_shape).reshape(-1, BZ),
            jnp.broadcast_to(along_y[None, :, None, None], node_shape).reshape(-1, BZ),
            jnp.broadcast_to(height[None, None, :, :], node_shape).reshape(-1, BZ),
        ]
    )
    return (along_x, along_y, along_z, coords)


def spline_weights(position):
    along_x, along_y, along_z, coords = node_offsets()
    weight_x = spline(position[0][None] - along_x[:, None, None])
    weight_y = spline(position[1][None] - along_y[:, None, None])
    weight_z = spline(position[2][None] - along_z[:, None, None])
    joined = weight_x[:, None, None] * weight_y[None, :, None] * weight_z[None, None, :]
    return (joined.reshape(-1, BZ, joined.shape[3], joined.shape[4]), coords)


def brick_index(block_brick):
    cells = jnp.arange(BZ, dtype=jnp.int32)
    return block_brick[None, :] * BZ + cells[:, None]


def matrix_entry(matrix, row_index, column):
    return matrix[3 * row_index + column]


def particle_terms(position, velocity, affine, deform, weighed):
    determinant = (
        matrix_entry(deform, 0, 0)
        * (
            matrix_entry(deform, 1, 1) * matrix_entry(deform, 2, 2)
            - matrix_entry(deform, 1, 2) * matrix_entry(deform, 2, 1)
        )
        - matrix_entry(deform, 0, 1)
        * (
            matrix_entry(deform, 1, 0) * matrix_entry(deform, 2, 2)
            - matrix_entry(deform, 1, 2) * matrix_entry(deform, 2, 0)
        )
        + matrix_entry(deform, 0, 2)
        * (
            matrix_entry(deform, 1, 0) * matrix_entry(deform, 2, 1)
            - matrix_entry(deform, 1, 1) * matrix_entry(deform, 2, 0)
        )
    )
    log_volume = jnp.log(determinant)
    momentum_matrix = []
    for row_index in range(3):
        for column in range(3):
            product = sum(
                (
                    matrix_entry(deform, row_index, inner_axis)
                    * matrix_entry(deform, column, inner_axis)
                    for inner_axis in range(3)
                )
            )
            identity = 1.0 if row_index == column else 0.0
            kirchhoff = shear_modulus * (product - identity) + lame_first * log_volume * identity
            momentum_matrix.append(
                weighed * (matrix_entry(affine, row_index, column) - stress_factor * kirchhoff)
            )
    carried = [
        weighed * velocity[row_index]
        - sum(
            (
                momentum_matrix[3 * row_index + inner_axis] * position[inner_axis]
                for inner_axis in range(3)
            )
        )
        for row_index in range(3)
    ]
    return jnp.stack([weighed] + carried + momentum_matrix, axis=0)


def block_grids(weights, quantities, coords):
    block_totals = jnp.einsum("kbp,gcbp->kgcb", quantities, weights, precision=highest)
    momentum_rows = [
        block_totals[1 + row_index]
        + sum(
            (
                block_totals[4 + 3 * row_index + inner_axis] * coords[inner_axis][:, :, None]
                for inner_axis in range(3)
            )
        )
        for row_index in range(3)
    ]
    return jnp.stack([block_totals[0]] + momentum_rows, axis=0)


def bricks_to_grid(table, components):
    shaped = table.reshape(components, 2, BX, 2, BY, 2, NBX, NBY, GZ)
    total_grid = jnp.zeros((components, GX + BX, GY + BY, GZ + BZ), jnp.float32)
    for shift_x in (0, 1):
        for shift_y in (0, 1):
            for shift_z in (0, 1):
                brick_piece = shaped[:, shift_x, :, shift_y, :, shift_z]
                brick_piece = jnp.transpose(brick_piece, (0, 3, 1, 4, 2, 5)).reshape(
                    components, GX, GY, GZ
                )
                total_grid = total_grid + jnp.pad(
                    brick_piece,
                    (
                        (0, 0),
                        (shift_x * BX, (1 - shift_x) * BX),
                        (shift_y * BY, (1 - shift_y) * BY),
                        (shift_z * BZ, (1 - shift_z) * BZ),
                    ),
                )
    return total_grid


def grid_to_bricks(padded, components):
    pieces_x = []
    for shift_x in (0, 1):
        pieces_y = []
        for shift_y in (0, 1):
            pieces_z = []
            for shift_z in (0, 1):
                window = padded[
                    :,
                    shift_x * BX : shift_x * BX + GX,
                    shift_y * BY : shift_y * BY + GY,
                    shift_z * BZ : shift_z * BZ + GZ,
                ]
                window = window.reshape(components, NBX, BX, NBY, BY, GZ)
                pieces_z.append(jnp.transpose(window, (0, 2, 4, 1, 3, 5)))
            pieces_y.append(jnp.stack(pieces_z, axis=3))
        pieces_x.append(jnp.stack(pieces_y, axis=2))
    stacked = jnp.stack(pieces_x, axis=1)
    return stacked.reshape(components * 8 * BX * BY, NBX * NBY * GZ)


def live_mass(particle_mass, block_count):
    slot_index = lax.broadcasted_iota(jnp.int32, particle_mass.shape, 1)
    live_slots = (slot_index < block_count[:, None]).astype(jnp.float32)
    return (live_slots, particle_mass * live_slots)


def scatter_particles(position, velocity, affine, deform, particle_mass, block_count, block_brick):
    live_slots, weighed = live_mass(particle_mass, block_count)
    weights, coords = spline_weights(position)
    quantities = particle_terms(position, velocity, affine, deform, weighed)
    per_block = block_grids(weights, quantities, coords)
    flat = per_block.reshape(-1, BZ, per_block.shape[3])
    table = (
        jnp.zeros((flat.shape[0], NBX * NBY * GZ), jnp.float32)
        .at[:, brick_index(block_brick)]
        .add(flat)
    )
    return (bricks_to_grid(table, 4), weights, coords, live_slots, weighed)


def node_velocity(summed, boundary_mask):
    movable = (1 - boundary_mask).astype(jnp.float32)
    divisor = jnp.maximum(summed[0], mass_floor)
    return jnp.stack(
        [
            movable * (summed[1 + axis_index] / divisor + time_step * gravity[axis_index])
            for axis_index in range(3)
        ]
    )


def gather_particles(weights, coords, brick_velocity, position, deform, live_slots):
    rows_list = [brick_velocity[row_index] for row_index in range(3)]
    rows_list = rows_list + [
        brick_velocity[row_index] * coords[column][:, :, None]
        for row_index in range(3)
        for column in range(3)
    ]
    node_table = jnp.stack(rows_list, axis=0)
    result = jnp.einsum("gcbp,kgcb->kbp", weights, node_table, precision=highest)
    new_velocity = [result[row_index] for row_index in range(3)]
    new_affine = [
        4.0 * (result[3 + 3 * row_index + column] - new_velocity[row_index] * position[column])
        for row_index in range(3)
        for column in range(3)
    ]
    new_deform = []
    for row_index in range(3):
        for column in range(3):
            advanced = deform[3 * row_index + column] + time_step * sum(
                (
                    new_affine[3 * row_index + inner_axis] * deform[3 * inner_axis + column]
                    for inner_axis in range(3)
                )
            )
            new_deform.append(advanced)
    new_position = [
        position[row_index] + time_step * new_velocity[row_index] for row_index in range(3)
    ]
    return jnp.stack(new_position + new_velocity + new_affine + new_deform) * live_slots


def fetch_bricks(padded, block_brick):
    table = grid_to_bricks(padded, 3)
    fetched = jnp.take(table, brick_index(block_brick), axis=1)
    return fetched.reshape(3, -1, BZ, block_brick.shape[0])


def outgoing_blocks(carried_state, leaving_block, leaving_dest):
    labels = jnp.arange(9, dtype=jnp.int32)
    onehot = (leaving_dest[:, None] == labels[None, :]).astype(jnp.int32)
    earlier = jnp.cumsum(onehot, axis=0) - onehot
    entry_rank = jnp.sum(earlier * onehot, axis=1)
    slot_index = jnp.arange(8 * MIG, dtype=jnp.int32)
    move_index = slot_index // MIG
    wanted = move_index + (move_index >= 4).astype(jnp.int32)
    matches = (leaving_dest[None, :] == wanted[:, None]) & (
        entry_rank[None, :] == (slot_index % MIG)[:, None]
    )
    source = jnp.sum(matches.astype(jnp.int32) * leaving_block[None, :], axis=1)
    present = jnp.any(matches, axis=1).astype(jnp.float32)
    return jnp.take(carried_state, source, axis=1) * present[None, :, None]


def staying_blocks(leaving_block, leaving_dest, blocks):
    hit_table = (leaving_block[:, None] == jnp.arange(blocks, dtype=jnp.int32)[None, :]) & (
        leaving_dest[:, None] != 4
    )
    return 1.0 - jnp.any(hit_table, axis=0).astype(jnp.float32)


def fold_down(partial_value):
    arrived_rim = passed_along(partial_value[:, GX:], "down", 1)
    return jnp.concatenate([partial_value[:, :BX] + arrived_rim, partial_value[:, BX:GX]], axis=1)


def fold_cross(partial_value):
    arrived_rim = passed_along(partial_value[:, :, GY:], "cross", 1)
    return jnp.concatenate(
        [partial_value[:, :, :BY] + arrived_rim, partial_value[:, :, BY:GY]], axis=2
    )


def extend_down(node_field):
    from_next = passed_along(node_field[:, :BX], "down", -1)
    return jnp.concatenate([node_field, from_next], axis=1)


def extend_cross(node_field):
    from_next = passed_along(node_field[:, :, :BY], "cross", -1)
    return jnp.concatenate([node_field, from_next], axis=2)


def body(
    position,
    velocity,
    affine,
    deform,
    particle_mass,
    block_count,
    block_brick,
    boundary_mask,
    leaving_block,
    leaving_dest,
):
    local_grid, weights, coords, live_slots, weighed = scatter_particles(
        position, velocity, affine, deform, particle_mass, block_count, block_brick
    )
    partial_value = local_grid[:, :, :, :GZ]
    summed = fold_down(fold_cross(partial_value))
    node_field = node_velocity(summed, boundary_mask)
    extended = extend_cross(extend_down(node_field))
    padded = jnp.pad(extended, ((0, 0), (0, 0), (0, 0), (0, BZ)))
    brick_velocity = fetch_bricks(padded, block_brick)
    updated = gather_particles(weights, coords, brick_velocity, position, deform, live_slots)
    staying = staying_blocks(leaving_block, leaving_dest, updated.shape[1])
    new_state = updated * staying[None, :, None]
    carried_state = jnp.concatenate([updated, weighed[None]], axis=0)
    outgoing = outgoing_blocks(carried_state, leaving_block, leaving_dest).reshape(
        25, 8, MIG, SLOTS
    )
    arrived = [outgoing[:, move_index] for move_index in range(8)]
    for step_down, first_member in ((-1, 0), (1, 5)):
        send_group = outgoing[:, first_member : first_member + 3]
        moved_group = passed_along(send_group, "down", step_down)
        for offset_index in range(3):
            arrived[first_member + offset_index] = moved_group[:, offset_index]
    for step_cross in (-1, 1):
        members = [move_index for move_index, move in enumerate(move_list) if move[1] == step_cross]
        send_group = jnp.stack([arrived[member] for member in members], axis=1)
        moved_group = passed_along(send_group, "cross", step_cross)
        for offset_index, member in enumerate(members):
            arrived[member] = moved_group[:, offset_index]
    arrivals = jnp.stack(arrived, axis=1).reshape(25, 8 * MIG, SLOTS)
    return (new_state, arrivals)


def solution(mesh):
    in_specs = (
        P(None, ("down", "cross"), None),
        P(None, ("down", "cross"), None),
        P(None, ("down", "cross"), None),
        P(None, ("down", "cross"), None),
        P(("down", "cross"), None),
        P(("down", "cross")),
        P(("down", "cross")),
        P("down", "cross", None),
        P(("down", "cross")),
        P(("down", "cross")),
    )
    out_specs = (P(None, ("down", "cross"), None), P(None, ("down", "cross"), None))
    return jax.shard_map(body, mesh=mesh, in_specs=in_specs, out_specs=out_specs, check_vma=False)
```

profile of v0, /device:TPU:21, one launch (start us, length us, event | category | flops | bytes accessed | tf_op | source)
XLA Modules:
  0.0 179.0 jit_solution(8824694517010066382)
XLA Ops:
  0.6 0.8 slice_bitcast_fusion.10
  1.5 1.1 fusion.47
  2.7 1.0 fusion.51
  3.7 1.0 fusion.98
  4.8 2.5 %broadcast_multiply_fusion = f32[4,4,8,64,128]{4,3,2,1,0:T(8,128)} fusion(f32[8,64,128]{2,1,0:T(8,128)S(1)} %multiply_select_fusion, f32[4,4,64,128]{3,2,1,0:T(8,128)S(1)} %broadcast_multiply_fusion.3), kind=kLoop, calls=%fused_computation.8 | loop fusion | flops 1048576 | bytes 4980736 | tf_op jit(solution)/shard_map/mul | solution.py:64
  7.2 0.6 stack.208
  7.9 19.5 %fusion.2 = f32[64,32,4,13]{1,3,2,0:T(8,128)S(1)} fusion(f32[32,4,64,128]{3,2,1,0:T(8,128)} %bitcast.517, f32[13,64,128]{2,0,1:T(8,128)S(1)} %stack.208), kind=kOutput, calls=%fused_computation.5 | convolution fusion | flops 163577856 | bytes 5046272 | tf_op jit(solution)/shard_map/kbp,gcbp->kgcb/dot_general | solution.py:125
  27.4 1.1 copy.263
  28.9 0.1 fusion.33
  29.1 0.1 copy.266
  29.3 3.6 %scatter_custom_fusion = f32[128,8192]{0,1:T(8,128)} fusion(s32[256]{0:T(256)S(1)} %reshape.329, f32[256,128]{1,0:T(8,128)S(1)} %bitcast.591, f32[]{:T(128)} %constant.58.clone.1), kind=kCustom, calls=%fused_computation.9 | custom fusion | flops 32768 | bytes 4194308 | tf_op jit(solution)/shard_map/scatter-add | solution.py:197
  33.0 5.6 %copy.267 = f32[128,8192]{1,0:T(8,128)} copy(f32[128,8192]{0,1:T(8,128)} %scatter_custom_fusion) | data formatting | bytes 8388608 | tf_op jit(solution)/shard_map/scatter-add | solution.py:197
  38.6 2.9 %copy.305 = f32[16,8,64,128]{3,2,1,0:T(8,128)S(1)} copy(f32[16,8,64,128]{3,1,2,0:T(8,128)} %bitcast.520) | data formatting | bytes 8388608
  41.6 0.6 slice_bitcast_fusion.7
  42.1 0.4 copy.268
  42.6 0.4 copy.269
  43.0 0.4 copy.270
  43.4 0.4 copy.271
  43.8 0.4 copy.272
  44.2 0.4 copy.273
  44.6 0.4 copy.274
  45.0 0.4 copy.275
  45.5 1.4 pad_add_fusion
  47.0 8.9 %collective-permute-start = (f32[4,18,2,128]{3,2,1,0:T(2,128)S(1)}, f32[4,18,2,128]{3,2,1,0:T(2,128)S(1)}, u32[]{:S(2)}, u32[]{:S(2)}) collective-permute-start(f32[4,18,2,128]{3,2,1,0:T(2,128)S(1)} %slice.559), channel_id=1, source_target_pairs={{0,1},{1,2},{2,3},{3,4},{4,5},{5,6},{6,7},{8,9},{9,10},{10,11},{11... | collective-permute-start | bytes 221192 | tf_op jit(solution)/shard_map/ppermute | solution.py:31
  56.3 0.2 select_reduce_fusion.1
  56.5 0.2 select_reduce_fusion
  56.8 0.1 copy.249
  56.9 0.1 fusion.103
  57.0 0.2 fusion.104
  57.3 0.4 collective-permute-done
  57.7 4.7 %collective-permute-start.1 = (f32[4,2,16,128]{3,2,1,0:T(8,128)S(1)}, f32[4,2,16,128]{3,2,1,0:T(8,128)S(1)}, u32[]{:S(2)}, u32[]{:S(2)}) collective-permute-start(f32[4,2,16,128]{3,2,1,0:T(8,128)S(1)} %pad_maximum_fusion.9), channel_id=1, source_target_pairs={{0,8},{8,16},{16,24},{24,32},{32,40},{40,48},{48,56},{56,64},{64,7... | collective-permute-start | bytes 196616 | tf_op jit(solution)/shard_map/ppermute | solution.py:31
  62.5 1.3 collective-permute-done.1
  63.9 6.7 %collective-permute-start.2 = (f32[3,2,16,128]{3,2,1,0:T(8,128)S(1)}, f32[3,2,16,128]{3,2,1,0:T(8,128)S(1)}, u32[]{:S(2)}, u32[]{:S(2)}) collective-permute-start(f32[3,2,16,128]{3,2,1,0:T(8,128)S(1)} %pad_maximum_fusion.11), channel_id=1, source_target_pairs={{8,0},{16,8},{24,16},{32,24},{40,32},{48,40},{56,48},{64,56},{72,6... | collective-permute-start | bytes 147464 | tf_op jit(solution)/shard_map/ppermute | solution.py:31
  70.7 0.2 maximum_bitcast_fusion.6
  71.0 0.6 collective-permute-done.2
  71.6 8.2 %collective-permute-start.3 = (f32[3,18,2,128]{3,2,1,0:T(2,128)S(1)}, f32[3,18,2,128]{3,2,1,0:T(2,128)S(1)}, u32[]{:S(2)}, u32[]{:S(2)}) collective-permute-start(f32[3,18,2,128]{3,2,1,0:T(2,128)S(1)} %pad_maximum_fusion.10), channel_id=1, source_target_pairs={{1,0},{2,1},{3,2},{4,3},{5,4},{6,5},{7,6},{9,8},{10,9},{11,10},{12... | collective-permute-start | bytes 165896 | tf_op jit(solution)/shard_map/ppermute | solution.py:31
  79.8 1.3 collective-permute-done.3
  81.2 0.5 pad_slice_fusion.3
  82.1 0.1 maximum_bitcast_fusion
  82.3 0.1 maximum_bitcast_fusion.1
  82.4 0.4 pad_maximum_fusion
  82.8 1.9 %copy.284 = f32[3,2,2,2,2,2,8,8,128]{8,7,6,5,4,3,2,1,0:T(8,128)} copy(f32[3,2,2,2,2,2,8,8,128]{8,7,6,4,2,0,5,3,1:T(8,128)S(1)} %pad_maximum_fusion) | data formatting | bytes 6291456 | tf_op jit(solution)/shard_map/stack | solution.py:178
  84.7 2.9 %reshape.308 = f32[96,8192]{1,0:T(8,128)S(1)} reshape(f32[3,2,2,2,2,2,8,8,128]{8,7,6,5,4,3,2,1,0:T(8,128)} %copy.284) | data formatting | bytes 6291456 | tf_op jit(solution)/shard_map/reshape | solution.py:179
  87.6 3.4 %copy.285 = f32[96,8192]{0,1:T(8,128)} copy(f32[96,8192]{1,0:T(8,128)S(1)} %reshape.308) | data formatting | bytes 6291456 | tf_op jit(solution)/shard_map/reshape | solution.py:179
  91.0 2.9 %gather_fusion = f32[256,96]{1,0:T(8,128)S(1)} fusion(f32[96,8192]{0,1:T(8,128)} %copy.285, s32[1024]{0:T(1024)S(1)} %get-tuple-element.92), kind=kCustom, calls=%fused_computation | custom fusion | bytes 197632 | tf_op jit(solution)/shard_map/jit(_take)/gather | solution.py:246
  93.9 0.1 fusion.21
  94.1 0.9 broadcast_multiply_fusion.4
  95.0 3.6 %stack.248 = f32[12,32,4,64]{1,0,2,3:T(8,128)S(1)} concatenate(f32[1,32,4,64]{1,0,2,3:T(1,128)} %bitcast.590, f32[1,32,4,64]{1,0,2,3:T(1,128)} %bitcast.589, f32[1,32,4,64]{1,0,2,3:T(1,128)S(1)} %bitcast.588, f32[1,32,4,64]{1,0,2,3:T(1,128)S(1)} %bitcast.582, f32[1,32,4,64]{1,0,2,3:T(1,128)S(1)} %bitcast.585, f32[1,32,4,64]{1,0,2,3:T(1,128)S(1)} %bitcast.581, ...), dimensions={0} | concatenate | bytes 786432 | tf_op jit(solution)/shard_map/stack | solution.py:220
  98.6 9.5 %fusion.6 = f32[64,12,128]{2,1,0:T(8,128)S(1)} fusion(f32[12,32,4,64]{1,0,2,3:T(8,128)S(1)} %stack.248, f32[32,4,64,128]{3,2,1,0:T(8,128)} %bitcast.518), kind=kOutput, calls=%fused_computation.18 | convolution fusion | flops 150994944 | bytes 4980736 | tf_op jit(solution)/shard_map/gcbp,kgcb->kbp/dot_general | solution.py:221
  108.1 0.1 copy.326
  108.5 0.6 copy-done
  109.3 1.1 broadcast_multiply_fusion.1
  110.4 0.5 copy.301
  110.9 0.6 gather_fusion.1
  111.6 0.2 select_multiply_fusion
  111.8 1.9 %collective-permute-start.5 = (f32[25,3,8,128]{3,0,2,1:T(8,128)S(1)}, f32[25,3,8,128]{3,0,2,1:T(8,128)S(1)}, u32[]{:S(2)}, u32[]{:S(2)}) collective-permute-start(f32[25,3,8,128]{3,0,2,1:T(8,128)S(1)} %get-tuple-element.50), channel_id=1, source_target_pairs={{0,8},{8,16},{16,24},{24,32},{32,40},{40,48},{48,56},{56,64},{64,7... | collective-permute-start | bytes 921608 | tf_op jit(solution)/shard_map/ppermute | solution.py:31
  113.8 3.7 %collective-permute-start.4 = (f32[25,3,8,128]{3,0,2,1:T(8,128)S(1)}, f32[25,3,8,128]{3,0,2,1:T(8,128)S(1)}, u32[]{:S(2)}, u32[]{:S(2)}) collective-permute-start(f32[25,3,8,128]{3,0,2,1:T(8,128)S(1)} %get-tuple-element.49), channel_id=1, source_target_pairs={{8,0},{16,8},{24,16},{32,24},{40,32},{48,40},{56,48},{64,56},{72,6... | collective-permute-start | bytes 921608 | tf_op jit(solution)/shard_map/ppermute | solution.py:31
  117.5 1.0 collective-permute-done.5
  118.5 8.9 %collective-permute-done.4 = f32[25,3,8,128]{3,0,2,1:T(8,128)S(1)} collective-permute-done((f32[25,3,8,128]{3,0,2,1:T(8,128)S(1)}, f32[25,3,8,128]{3,0,2,1:T(8,128)S(1)}, u32[]{:S(2)}, u32[]{:S(2)}) %collective-permute-start.4) | collective-permute-done | bytes 307232 | tf_op jit(solution)/shard_map/ppermute | solution.py:31
  127.4 7.6 %collective-permute-start.6 = (f32[25,3,8,128]{3,0,2,1:T(8,128)S(1)}, f32[25,3,8,128]{3,0,2,1:T(8,128)S(1)}, u32[]{:S(2)}, u32[]{:S(2)}) collective-permute-start(f32[25,3,8,128]{3,0,2,1:T(8,128)S(1)} %pad_maximum_fusion.6), channel_id=1, source_target_pairs={{1,0},{2,1},{3,2},{4,3},{5,4},{6,5},{7,6},{9,8},{10,9},{11,10},{12... | collective-permute-start | bytes 921608 | tf_op jit(solution)/shard_map/ppermute | solution.py:31
  135.0 18.8 %collective-permute-done.6 = f32[25,3,8,128]{3,0,2,1:T(8,128)S(1)} collective-permute-done((f32[25,3,8,128]{3,0,2,1:T(8,128)S(1)}, f32[25,3,8,128]{3,0,2,1:T(8,128)S(1)}, u32[]{:S(2)}, u32[]{:S(2)}) %collective-permute-start.6) | collective-permute-done | bytes 307232 | tf_op jit(solution)/shard_map/ppermute | solution.py:31
  153.9 7.3 %collective-permute-start.7 = (f32[25,3,8,128]{3,0,2,1:T(8,128)S(1)}, f32[25,3,8,128]{3,0,2,1:T(8,128)S(1)}, u32[]{:S(2)}, u32[]{:S(2)}) collective-permute-start(f32[25,3,8,128]{3,0,2,1:T(8,128)S(1)} %pad_maximum_fusion.7), channel_id=1, source_target_pairs={{0,1},{1,2},{2,3},{3,4},{4,5},{5,6},{6,7},{8,9},{9,10},{10,11},{11... | collective-permute-start | bytes 921608 | tf_op jit(solution)/shard_map/ppermute | solution.py:31
  161.3 16.3 %collective-permute-done.7 = f32[25,3,8,128]{3,0,2,1:T(8,128)S(1)} collective-permute-done((f32[25,3,8,128]{3,0,2,1:T(8,128)S(1)}, f32[25,3,8,128]{3,0,2,1:T(8,128)S(1)}, u32[]{:S(2)}, u32[]{:S(2)}) %collective-permute-start.7) | collective-permute-done | bytes 307232 | tf_op jit(solution)/shard_map/ppermute | solution.py:31
  177.6 1.4 copy.325
  (103 shorter events, 2.7 us)
Async XLA Ops:
  27.4 1.8 %copy-start.6 = (s32[64]{0:T(128)S(1)}, s32[64]{0:T(128)}, u32[]{:S(2)}) copy-start(s32[64]{0:T(128)} %param.16) | copy-start | bytes 772
  45.5 10.6 %copy-start.4 = (s32[64]{0:T(128)S(1)}, s32[64]{0:T(128)}, u32[]{:S(2)}) copy-start(s32[64]{0:T(128)} %param.15) | copy-start | bytes 772
  45.5 10.7 %copy-start.3 = (s32[64]{0:T(128)S(1)}, s32[64]{0:T(128)}, u32[]{:S(2)}) copy-start(s32[64]{0:T(128)} %param.19) | copy-start | bytes 772
  45.5 11.0 %copy-start.5 = (s32[64]{0:T(128)S(1)}, s32[64]{0:T(128)}, u32[]{:S(2)}) copy-start(s32[64]{0:T(128)} %param.18) | copy-start | bytes 772
  47.0 16.9 %copy-start.2 = (s32[16,16,128]{2,1,0:T(8,128)S(1)}, s32[16,16,128]{2,1,0:T(8,128)}, u32[]{:S(2)}) copy-start(s32[16,16,128]{2,1,0:T(8,128)} %param.17) | copy-start | bytes 393220
  47.0 10.7 %collective-permute-start = (f32[4,18,2,128]{3,2,1,0:T(2,128)S(1)}, f32[4,18,2,128]{3,2,1,0:T(2,128)S(1)}, u32[]{:S(2)}, u32[]{:S(2)}) collective-permute-start(f32[4,18,2,128]{3,2,1,0:T(2,128)S(1)} %slice.559), channel_id=1, source_target_pairs={{0,1},{1,2},{2,3},{3,4},{4,5},{5,6},{6,7},{8,9},{9,10},{10,11},{11... | collective-permute-start | bytes 221192 | tf_op jit(solution)/shard_map/ppermute | solution.py:31
  57.7 6.0 %collective-permute-start.1 = (f32[4,2,16,128]{3,2,1,0:T(8,128)S(1)}, f32[4,2,16,128]{3,2,1,0:T(8,128)S(1)}, u32[]{:S(2)}, u32[]{:S(2)}) collective-permute-start(f32[4,2,16,128]{3,2,1,0:T(8,128)S(1)} %pad_maximum_fusion.9), channel_id=1, source_target_pairs={{0,8},{8,16},{16,24},{24,32},{32,40},{40,48},{48,56},{56,64},{64,7... | collective-permute-start | bytes 196616 | tf_op jit(solution)/shard_map/ppermute | solution.py:31
  63.9 7.6 %collective-permute-start.2 = (f32[3,2,16,128]{3,2,1,0:T(8,128)S(1)}, f32[3,2,16,128]{3,2,1,0:T(8,128)S(1)}, u32[]{:S(2)}, u32[]{:S(2)}) collective-permute-start(f32[3,2,16,128]{3,2,1,0:T(8,128)S(1)} %pad_maximum_fusion.11), channel_id=1, source_target_pairs={{8,0},{16,8},{24,16},{32,24},{40,32},{48,40},{56,48},{64,56},{72,6... | collective-permute-start | bytes 147464 | tf_op jit(solution)/shard_map/ppermute | solution.py:31
  71.6 9.5 %collective-permute-start.3 = (f32[3,18,2,128]{3,2,1,0:T(2,128)S(1)}, f32[3,18,2,128]{3,2,1,0:T(2,128)S(1)}, u32[]{:S(2)}, u32[]{:S(2)}) collective-permute-start(f32[3,18,2,128]{3,2,1,0:T(2,128)S(1)} %pad_maximum_fusion.10), channel_id=1, source_target_pairs={{1,0},{2,1},{3,2},{4,3},{5,4},{6,5},{7,6},{9,8},{10,9},{11,10},{12... | collective-permute-start | bytes 165896 | tf_op jit(solution)/shard_map/ppermute | solution.py:31
  98.6 9.6 %copy-start.1 = (f32[3,64,128]{2,1,0:T(8,128)S(1)}, f32[3,64,128]{2,1,0:T(8,128)}, u32[]{:S(2)}) copy-start(f32[3,64,128]{2,1,0:T(8,128)} %param.10) | copy-start | bytes 294916
  108.1 1.0 copy-start
  111.8 6.6 %collective-permute-start.5 = (f32[25,3,8,128]{3,0,2,1:T(8,128)S(1)}, f32[25,3,8,128]{3,0,2,1:T(8,128)S(1)}, u32[]{:S(2)}, u32[]{:S(2)}) collective-permute-start(f32[25,3,8,128]{3,0,2,1:T(8,128)S(1)} %get-tuple-element.50), channel_id=1, source_target_pairs={{0,8},{8,16},{16,24},{24,32},{32,40},{40,48},{48,56},{56,64},{64,7... | collective-permute-start | bytes 921608 | tf_op jit(solution)/shard_map/ppermute | solution.py:31
  113.8 13.6 %collective-permute-start.4 = (f32[25,3,8,128]{3,0,2,1:T(8,128)S(1)}, f32[25,3,8,128]{3,0,2,1:T(8,128)S(1)}, u32[]{:S(2)}, u32[]{:S(2)}) collective-permute-start(f32[25,3,8,128]{3,0,2,1:T(8,128)S(1)} %get-tuple-element.49), channel_id=1, source_target_pairs={{8,0},{16,8},{24,16},{32,24},{40,32},{48,40},{56,48},{64,56},{72,6... | collective-permute-start | bytes 921608 | tf_op jit(solution)/shard_map/ppermute | solution.py:31
  127.4 26.4 %collective-permute-start.6 = (f32[25,3,8,128]{3,0,2,1:T(8,128)S(1)}, f32[25,3,8,128]{3,0,2,1:T(8,128)S(1)}, u32[]{:S(2)}, u32[]{:S(2)}) collective-permute-start(f32[25,3,8,128]{3,0,2,1:T(8,128)S(1)} %pad_maximum_fusion.6), channel_id=1, source_target_pairs={{1,0},{2,1},{3,2},{4,3},{5,4},{6,5},{7,6},{9,8},{10,9},{11,10},{12... | collective-permute-start | bytes 921608 | tf_op jit(solution)/shard_map/ppermute | solution.py:31
  153.9 23.6 %collective-permute-start.7 = (f32[25,3,8,128]{3,0,2,1:T(8,128)S(1)}, f32[25,3,8,128]{3,0,2,1:T(8,128)S(1)}, u32[]{:S(2)}, u32[]{:S(2)}) collective-permute-start(f32[25,3,8,128]{3,0,2,1:T(8,128)S(1)} %pad_maximum_fusion.7), channel_id=1, source_target_pairs={{0,1},{1,2},{2,3},{3,4},{4,5},{5,6},{6,7},{8,9},{9,10},{10,11},{11... | collective-permute-start | bytes 921608 | tf_op jit(solution)/shard_map/ppermute | solution.py:31
where the time goes:
time: 180 us; the launch traced here: 179 us
  starting transfers between devices  49.1 us (27%)
  waiting for transfers between devices  48.5 us (27%)
  local copies, waits for them, and re-layouts  34.7 us (19%)
  matrix products  29 us (16%)
  other arithmetic  16.1 us (9%)
    ppermute x8, starting transfers between devices, passed_along(): lax.ppermute(value, axis, [(source, source + steps) for source in range(l...  49.1 us
    ppermute x8, waiting for transfers between devices, passed_along(): lax.ppermute(value, axis, [(source, source + steps) for source in range(l...  48.5 us
    dot_general x1, matrix products, block_grids(): jnp.einsum('kbp,gcbp->kgcb', quantities, weights, precision=highest)  19.5 us
    dot_general x1, matrix products, gather_particles(): jnp.einsum('gcbp,kgcb->kbp', weights, node_table, precision=highest)  9.45 us
    reshape x2, local copies, waits for them, and re-layouts, grid_to_bricks(): return stacked.reshape(components * 8 * BX * BY, NBX * NBY * GZ)  6.3 us
    scatter-add x1, local copies, waits for them, and re-layouts, scatter_particles(): table = jnp.zeros((flat.shape[0], NBX * NBY * GZ), jnp.float32).at[:, bri...  5.64 us
    transpose x9, local copies, waits for them, and re-layouts, bricks_to_grid(): jnp.transpose(brick_piece, (0, 3, 1, 4, 2, 5))  3.83 us
    scatter-add x1, other arithmetic, scatter_particles(): table = jnp.zeros((flat.shape[0], NBX * NBY * GZ), jnp.float32).at[:, bri...  3.64 us
  transfers between devices with their start and end apart: 8, of which 8 were waited for; matrix products, arithmetic and copies ran while one was open for 1% of the time, Pallas kernels for 0%

commit v1 on v0

v1 whole, which is shorter than its diff:
```python
import functools

import jax
import jax.numpy as jnp
from jax import lax
from jax.experimental import pallas as pl
from jax.experimental.pallas import tpu as pltpu
from jax.sharding import PartitionSpec as P

GX = 16
GY = 16
GZ = 128
SLOTS = 128
BLOCKS = 64
MIG = 8
NBX = 8
NBY = 8

time_step = 0.05
shear_modulus = 8.0
lame_first = 12.0
stress_factor = 0.2
gravity = (2.0, 0.0, -9.0)
mass_floor = 1.0
move_list = ((-1, -1), (-1, 0), (-1, 1), (0, -1), (0, 1), (1, -1), (1, 0), (1, 1))
early_order = (0, 2, 5, 7, 3, 4, 1, 6)
early_first = 4

MESH = pl.DeviceIdType.MESH
f32 = jnp.float32
bf16 = jnp.bfloat16


def spline(distance):
    magnitude = jnp.abs(distance)
    outer_part = jnp.maximum(1.5 - magnitude, 0.0)
    return jnp.where(magnitude < 0.5, 0.75 - magnitude * magnitude, 0.5 * outer_part * outer_part)


def row_iota(rows):
    return lax.broadcasted_iota(jnp.int32, (rows, 128), 0)


def lane_iota(rows):
    return lax.broadcasted_iota(jnp.int32, (rows, 128), 1)


def plane_weights(x0, x1):
    parity = (row_iota(8) & 1).astype(f32)
    dx = [float(x) - x0 for x in range(4)]
    wx = [spline(d) for d in dx]
    dy = [(parity + 2.0 * yp) - x1 for yp in range(2)]
    wy = [spline(d) for d in dy]
    return dx, wx, dy, wy


def split(value):
    high = value.astype(bf16)
    low = (value - high.astype(f32)).astype(bf16)
    return high, low


def particle_rows(deform, affine, velocity, mass):
    d = deform
    determinant = (
        d[0] * (d[4] * d[8] - d[5] * d[7])
        - d[1] * (d[3] * d[8] - d[5] * d[6])
        + d[2] * (d[3] * d[7] - d[4] * d[6])
    )
    pressure = lame_first * jnp.log(determinant)
    columns = [[None] * 3 for _ in range(3)]
    for a in range(3):
        for c in range(a, 3):
            product = d[3 * a] * d[3 * c] + d[3 * a + 1] * d[3 * c + 1] + d[3 * a + 2] * d[3 * c + 2]
            if a == c:
                tau = shear_modulus * (product - 1.0) + pressure
            else:
                tau = shear_modulus * product
            columns[c][a] = mass * (affine[3 * a + c] - stress_factor * tau)
            if a != c:
                columns[a][c] = mass * (affine[3 * c + a] - stress_factor * tau)
    return [mass] + [mass * v for v in velocity], columns


def gathered(lhs_f32, x0, x1, x2, limit):
    lane = lane_iota(64)
    high = lhs_f32.astype(bf16).astype(f32)
    low = lhs_f32 - high
    lhs = jnp.where((lane >= 8) & (lane < 16), low, high)
    lhs = jnp.where(lane < 24, lhs, 0.0).astype(bf16)
    height = row_iota(8)
    dz = height.astype(f32) - x2
    wz = spline(dz)
    if limit is not None:
        wz = jnp.where(height < limit, wz, 0.0)
    rhs = jnp.concatenate([wz, wz * dz], axis=1)
    rhs_high = rhs.astype(bf16).astype(f32)
    rhs_low = rhs - rhs_high
    stacked = jnp.concatenate([rhs_high, rhs_high, rhs_low, jnp.zeros_like(rhs)], axis=0).astype(bf16)
    u = jnp.dot(lhs[:, :32], stacked, preferred_element_type=f32)
    dx, wx, dy, wy = plane_weights(x0, x1)
    wyd = [w * d for w, d in zip(wy, dy)]
    total = None
    for x in range(4):
        a = b = c = None
        for yp in range(2):
            start = 8 * (2 * x + yp)
            u0 = u[start : start + 8, :128]
            u1 = u[start : start + 8, 128:]
            terms = (wy[yp] * u0, wyd[yp] * u0, wy[yp] * u1)
            a, b, c = terms if a is None else (a + terms[0], b + terms[1], c + terms[2])
        parts = (wx[x] * a, (wx[x] * dx[x]) * a, wx[x] * b, wx[x] * c)
        total = parts if total is None else tuple(t + p for t, p in zip(total, parts))
    return total


def final_rows(sums_ref, base, position, deform):
    def both(row):
        return sums_ref[pl.ds(base + row, 8, stride=32), :] + sums_ref[pl.ds(base + row + 1, 8, stride=32), :]

    v = [both(2 + 2 * a) for a in range(3)]
    c = [4.0 * both(8 * (1 + col) + 2 + 2 * a) for a in range(3) for col in range(3)]
    x = [position[a] + time_step * v[a] for a in range(3)]
    f = []
    for a in range(3):
        for col in range(3):
            grown = c[3 * a] * deform[col] + c[3 * a + 1] * deform[3 + col] + c[3 * a + 2] * deform[6 + col]
            f.append(deform[3 * a + col] + time_step * grown)
    return x + v + c + f


def kernel(
    n_down,
    n_cross,
    next_ref,
    first_ref,
    column_ref,
    lift_ref,
    source_ref,
    pos_ref,
    vel_ref,
    aff_ref,
    def_ref,
    mass_ref,
    present_ref,
    stay_ref,
    mask_ref,
    state_ref,
    arrive_ref,
    early,
    early_in,
    late,
    late_in,
    table,
    chain,
    grid,
    node_v,
    movable,
    mask_y,
    mask_x_in,
    mask_y_in,
    mask_c_in,
    face_x,
    face_y,
    corner,
    sums,
    early_send,
    early_recv,
    late_send,
    late_recv,
    halo_send,
    halo_recv,
    mask_send,
    mask_recv,
):
    i = lax.axis_index("down")
    j = lax.axis_index("cross")

    def device(a, b):
        return (lax.rem(i + (a + n_down), n_down), lax.rem(j + (b + n_cross), n_cross))

    def inside(a, b):
        valid = None
        if a:
            valid = (i + a >= 0) & (i + a < n_down)
        if b:
            other = (j + b >= 0) & (j + b < n_cross)
            valid = other if valid is None else valid & other
        return valid.astype(f32)

    barrier = pltpu.get_barrier_semaphore()
    for a, b in move_list:
        pl.semaphore_signal(barrier, inc=1, device_id=device(a, b), device_id_type=MESH)

    for move in range(8):

        def pick(k, carry, move=move):
            source = source_ref[move * 8 + k]
            early[move, 0:3, pl.ds(k, 1), :] = pos_ref[:, pl.ds(source, 1), :]
            early[move, 3:12, pl.ds(k, 1), :] = def_ref[:, pl.ds(source, 1), :]
            early[move, 12, pl.ds(k, 1), :] = (
                mass_ref[pl.ds(source, 1), :] * present_ref[pl.ds(move * 8 + k, 1), :]
            )
            return carry

        lax.fori_loop(0, 8, pick, 0)
    for par in range(2):
        mask_y[par] = mask_ref[pl.ds(par, 16, stride=16), :]

    def remote(source, target, send, recv, a, b):
        return pltpu.make_async_remote_copy(
            src_ref=source,
            dst_ref=target,
            send_sem=send,
            recv_sem=recv,
            device_id=device(a, b),
            device_id_type=MESH,
        )

    early_copies = [
        remote(early.at[m], early_in.at[m], early_send.at[m], early_recv.at[m], a, b)
        for m, (a, b) in enumerate(move_list)
    ]
    late_copies = [
        remote(late.at[m], late_in.at[m], late_send.at[m], late_recv.at[m], a, b)
        for m, (a, b) in enumerate(move_list)
    ]
    mask_copies = [
        remote(mask_y, mask_y_in, mask_send.at[0], mask_recv.at[0], 0, -1),
        remote(mask_ref.at[pl.ds(0, 32)], mask_x_in, mask_send.at[1], mask_recv.at[1], -1, 0),
        remote(mask_y.at[:, pl.ds(0, 8)], mask_c_in, mask_send.at[2], mask_recv.at[2], -1, -1),
    ]

    pl.semaphore_wait(barrier, 8)
    for copy in mask_copies:
        copy.start()
    for m in early_order[:early_first]:
        early_copies[m].start()

    def terms(g, carry):
        rows = pl.ds(pl.multiple_of(g * 8, 8), 8)
        deform = [def_ref[c, rows, :] for c in range(9)]
        affine = [aff_ref[c, rows, :] for c in range(9)]
        velocity = [vel_ref[c, rows, :] for c in range(3)]
        moved, columns = particle_rows(deform, affine, velocity, mass_ref[rows, :])
        zero = jnp.zeros((8, 128), f32)
        lists = [moved] + [[zero] + columns[c] for c in range(3)]
        for group, values in enumerate(lists):
            for quantity, value in enumerate(values):
                for par in range(2):
                    row = g * 256 + (8 * group + 2 * quantity + par)
                    table[pl.ds(row, 8, stride=32), :] = value
        return carry

    lax.fori_loop(0, 8, terms, 0)

    chain[BLOCKS] = jnp.zeros((64, 128), f32)

    def to_bricks(step, carry):
        b = (BLOCKS - 1) - step
        lift = lift_ref[b]
        x0 = pos_ref[0, pl.ds(b, 1), :]
        x1 = pos_ref[1, pl.ds(b, 1), :]
        x2 = pos_ref[2, pl.ds(b, 1), :]
        base = pl.multiple_of(b * 32, 32)
        moved = table[pl.ds(base, 8), :]
        col0 = table[pl.ds(base + 8, 8), :]
        col1 = table[pl.ds(base + 16, 8), :]
        col2 = table[pl.ds(base + 24, 8), :]
        dx, wx, dy, wy = plane_weights(x0, x1)
        plain, raised = [], []
        for x in range(4):
            at_x = moved + col0 * dx[x]
            for yp in range(2):
                weight = wx[x] * wy[yp]
                plain.append((at_x + col1 * dy[yp]) * weight)
                raised.append(col2 * weight)
        lhs = jnp.concatenate([jnp.concatenate(plain, axis=0), jnp.concatenate(raised, axis=0)], axis=1)
        lhs_high, lhs_low = split(lhs)
        height = row_iota(8)
        dz = height.astype(f32) - x2
        wz = jnp.where(height + lift < GZ, spline(dz), 0.0)
        rhs = jnp.concatenate([wz, wz * dz], axis=1)
        rhs_high = rhs.astype(bf16).astype(f32)
        stacked = jnp.concatenate([rhs_high, rhs - rhs_high], axis=0).astype(bf16)
        contract = (((1,), (1,)), ((), ()))
        found = lax.dot_general(lhs_high, stacked, contract, preferred_element_type=f32)
        found = found + lax.dot_general(lhs_low, stacked, contract, preferred_element_type=f32)
        wide = jnp.concatenate([found, jnp.zeros((64, 112), f32)], axis=1)
        folded = pltpu.roll(wide, lift, 1) + pltpu.roll(wide, (lift + 120) & 127, 1)
        lane = lane_iota(64)
        here = (lane >= lift) & (lane < lift + 8)
        chain[b] = jnp.where(here, folded, 0.0) + chain[next_ref[b]]
        return carry

    lax.fori_loop(0, BLOCKS, to_bricks, 0)

    def clear(x, carry):
        grid[x] = jnp.zeros((9, 8, 128), f32)
        return carry

    lax.fori_loop(0, 18, clear, 0)

    def spread(column, carry):
        p = column // NBY
        q = lax.rem(column, NBY)
        first = first_ref[column]
        for x in range(4):
            for yp in range(2):
                start = 8 * (2 * x + yp)
                grid[2 * p + x, q + yp] += chain[first, start : start + 8, :]
        return carry

    lax.fori_loop(0, NBX * NBY, spread, 0)

    halo_copies = []
    faces = {-1: 0, 1: 1}
    for m, (a, b) in enumerate(move_list):
        xs = pl.ds(16, 2) if a == 1 else pl.ds(0, 2)
        y = 8 if b == 1 else 0
        if b == 0:
            source, target = grid.at[xs], face_x.at[faces[a]]
        elif a == 0:
            source, target = grid.at[:, y], face_y.at[faces[b]]
        else:
            source, target = grid.at[xs, y], corner.at[2 * faces[a] + faces[b]]
        halo_copies.append(remote(source, target, halo_send.at[m], halo_recv.at[m], a, b))
    for m in (3, 4, 0, 2, 5, 7, 1, 6):
        halo_copies[m].start()
    for m in early_order[early_first:]:
        early_copies[m].start()

    def own_mask(x, carry):
        movable[x, 0:16, :] = (1 - mask_ref[pl.ds(pl.multiple_of(x * 16, 16), 16), :]).astype(f32)
        return carry

    lax.fori_loop(0, 16, own_mask, 0)
    row8 = row_iota(8)
    even = (row8 & 1) == 0
    quantity = row8 // 2
    pull = jnp.where(quantity == 1, time_step * gravity[0], 0.0)
    pull = jnp.where(quantity == 2, time_step * gravity[1], pull)
    pull = jnp.where(quantity == 3, time_step * gravity[2], pull)

    def put_velocity(x, yp, tile):
        mass = jnp.where(row8 < 2, tile, 0.0)
        mass = mass + pltpu.roll(mass, 2, 0)
        mass = mass + pltpu.roll(mass, 4, 0)
        free = jnp.where(even, movable[x, pl.ds(2 * yp, 1), :], movable[x, pl.ds(2 * yp + 1, 1), :])
        node_v[x, yp] = free * (tile / jnp.maximum(mass, mass_floor) + pull)

    def interior(x, carry):
        for yp in range(1, 8):
            put_velocity(x, yp, grid[x, yp])
        return carry

    lax.fori_loop(2, 16, interior, 0)
    for copy in mask_copies:
        copy.wait()
    past_x = inside(1, 0)
    past_y = inside(0, 1)
    past_c = inside(1, 1)
    for xx in range(2):
        movable[16 + xx, 0:16, :] = (1 - mask_x_in[pl.ds(16 * xx, 16), :]).astype(f32) * past_x
        for par in range(2):
            movable[16 + xx, 16 + par : 17 + par, :] = (
                1 - mask_c_in[par, xx : xx + 1, :]
            ).astype(f32) * past_c

    def side_mask(x, carry):
        for par in range(2):
            movable[x, 16 + par : 17 + par, :] = (1 - mask_y_in[par, pl.ds(x, 1), :]).astype(f32) * past_y
        return carry

    lax.fori_loop(0, 16, side_mask, 0)
    for copy in halo_copies:
        copy.wait()
    has = {(a, b): inside(-a, -b) for a, b in move_list}

    def low_high(yp):
        for a in (-1, 1):
            for xx in range(2):
                x = xx if a == 1 else 16 + xx
                yield a, xx, x, grid[x, yp] + face_x[faces[a], xx, yp] * has[(a, 0)]

    def edge_x(yp, carry):
        for _, _, x, tile in low_high(yp):
            put_velocity(x, yp, tile)
        return carry

    lax.fori_loop(1, 8, edge_x, 0)

    def edge_y(x, carry):
        for b in (-1, 1):
            yp = 0 if b == 1 else 8
            put_velocity(x, yp, grid[x, yp] + face_y[faces[b], x] * has[(0, b)])
        return carry

    lax.fori_loop(2, 16, edge_y, 0)
    for b in (-1, 1):
        yp = 0 if b == 1 else 8
        for a, xx, x, tile in low_high(yp):
            tile = tile + face_y[faces[b], x] * has[(0, b)]
            tile = tile + corner[2 * faces[a] + faces[b], xx] * has[(a, b)]
            put_velocity(x, yp, tile)

    lane8 = lane_iota(8)

    def brick_tiles(b):
        column = column_ref[b]
        p = column // NBY
        q = lax.rem(column, NBY)
        return [node_v[2 * p + x, q + yp] for x in range(4) for yp in range(2)]

    for move in range(8):

        def window(k, carry, move=move):
            b = source_ref[move * 8 + k]
            lift = lift_ref[b]
            tiles = brick_tiles(b)
            shift = (8 * k - lift + 128) & 127
            local = lane8 - 8 * k
            low = (local >= 0) & (local < 8) & (local + lift < GZ)
            local = local - 64
            high = (local >= 0) & (local < 8) & (local + lift < GZ)
            out = []
            for t in range(4):
                kept = jnp.where(low, pltpu.roll(tiles[t], shift, 1), carry[t])
                out.append(jnp.where(high, pltpu.roll(tiles[t + 4], (shift + 64) & 127, 1), kept))
            return tuple(out)

        zero = jnp.zeros((8, 128), f32)
        packed = lax.fori_loop(0, 8, window, (zero,) * 4)
        for t in range(3):
            moved = pltpu.roll(packed[3], (8 - (2 + 2 * t)) & 7, 0)
            late[move, t] = jnp.where(row8 < 2, moved, packed[t])
        late_copies[move].start()

    lane64 = lane_iota(64)

    def windows(stack, shift):
        first = pltpu.roll(stack, shift & 127, 1)
        second = pltpu.roll(stack, (shift + 8) & 127, 1)
        third = pltpu.roll(stack, (shift + 16) & 127, 1)
        return jnp.where(lane64 < 8, first, jnp.where(lane64 < 16, second, third))

    def put_sums(b, total):
        base = pl.multiple_of(b * 32, 32)
        for t in range(4):
            sums[pl.ds(base + 8 * t, 8), :] = total[t]

    def resident(b, carry):
        lift = lift_ref[b]
        stack = jnp.concatenate(brick_tiles(b), axis=0)
        total = gathered(
            windows(stack, 128 - lift),
            pos_ref[0, pl.ds(b, 1), :],
            pos_ref[1, pl.ds(b, 1), :],
            pos_ref[2, pl.ds(b, 1), :],
            GZ - lift,
        )
        put_sums(b, total)
        return carry

    lax.fori_loop(0, BLOCKS, resident, 0)

    def finish(g, carry):
        rows = pl.ds(pl.multiple_of(g * 8, 8), 8)
        position = [pos_ref[c, rows, :] for c in range(3)]
        deform = [def_ref[c, rows, :] for c in range(9)]
        keep = jnp.where(mass_ref[rows, :] > 0.0, stay_ref[rows, :], 0.0)
        for row, value in enumerate(final_rows(sums, g * 256, position, deform)):
            state_ref[row, rows, :] = value * keep
        return carry

    lax.fori_loop(0, 8, finish, 0)

    for move, (a, b) in enumerate(move_list):
        early_copies[move].wait()
        late_copies[move].wait()
        packed = [late_in[move, t] for t in range(3)]
        last = jnp.zeros((8, 128), f32)
        for t in range(3):
            last = last + pltpu.roll(jnp.where(row8 < 2, packed[t], 0.0), 2 + 2 * t, 0)
        packed.append(last)
        low_stack = jnp.concatenate(packed, axis=0)
        stack = jnp.concatenate([low_stack, pltpu.roll(low_stack, 64, 1)], axis=0)

        def arriving(k, carry, move=move, stack=stack):
            total = gathered(
                windows(stack, 128 - 8 * k),
                early_in[move, 0, pl.ds(k, 1), :],
                early_in[move, 1, pl.ds(k, 1), :],
                early_in[move, 2, pl.ds(k, 1), :],
                None,
            )
            put_sums(k, total)
            return carry

        lax.fori_loop(0, 8, arriving, 0)
        rows = pl.ds(move * 8, 8)
        position = [early_in[move, c] for c in range(3)]
        deform = [early_in[move, 3 + c] for c in range(9)]
        mass = early_in[move, 12] * inside(-a, -b)
        keep = jnp.where(mass > 0.0, 1.0, 0.0)
        for row, value in enumerate(final_rows(sums, 0, position, deform)):
            arrive_ref[row, rows, :] = value * keep
        arrive_ref[24, rows, :] = mass


def brick_tables(block_brick):
    column = block_brick // 32
    ids = jnp.arange(BLOCKS, dtype=jnp.int32)
    later = (column[:, None] == column[None, :]) & (ids[None, :] > ids[:, None])
    following = jnp.min(jnp.where(later, ids[None, :], BLOCKS), axis=1)
    held = column[None, :] == jnp.arange(NBX * NBY, dtype=jnp.int32)[:, None]
    first = jnp.min(jnp.where(held, ids[None, :], BLOCKS), axis=1)
    return following, first, column, (block_brick % 32) * 4


def leaving_tables(leaving_block, leaving_dest):
    order = jnp.arange(BLOCKS, dtype=jnp.int32)
    ahead = (leaving_dest[:, None] == leaving_dest[None, :]) & (order[None, :] < order[:, None])
    entry_rank = jnp.sum(ahead.astype(jnp.int32), axis=1)
    slot_index = jnp.arange(8 * MIG, dtype=jnp.int32)
    move_index = slot_index // MIG
    wanted = move_index + (move_index >= 4).astype(jnp.int32)
    matches = (leaving_dest[None, :] == wanted[:, None]) & (entry_rank[None, :] == (slot_index % MIG)[:, None])
    source = jnp.sum(matches.astype(jnp.int32) * leaving_block[None, :], axis=1)
    present = jnp.any(matches, axis=1).astype(f32)
    hit_table = (leaving_block[:, None] == order[None, :]) & (leaving_dest[:, None] != 4)
    staying = 1.0 - jnp.any(hit_table, axis=0).astype(f32)
    return source, present, staying


def body(
    n_down,
    n_cross,
    position,
    velocity,
    affine,
    deform,
    particle_mass,
    block_count,
    block_brick,
    boundary_mask,
    leaving_block,
    leaving_dest,
):
    slot_index = lax.broadcasted_iota(jnp.int32, particle_mass.shape, 1)
    weighed = jnp.where(slot_index < block_count[:, None], particle_mass, 0.0)
    following, first, column, lift = brick_tables(block_brick)
    source, present, staying = leaving_tables(leaving_block, leaving_dest)
    wide = (BLOCKS, SLOTS)
    present = jnp.broadcast_to(present[:, None], wide)
    staying = jnp.broadcast_to(staying[:, None], wide)
    smem = pl.BlockSpec(memory_space=pltpu.SMEM)
    vmem = pl.BlockSpec(memory_space=pltpu.VMEM)
    dma = pltpu.SemaphoreType.DMA
    return pl.pallas_call(
        functools.partial(kernel, n_down, n_cross),
        out_shape=(
            jax.ShapeDtypeStruct((24, BLOCKS, SLOTS), f32),
            jax.ShapeDtypeStruct((25, BLOCKS, SLOTS), f32),
        ),
        in_specs=[smem] * 5 + [vmem] * 8,
        out_specs=(vmem, vmem),
        scratch_shapes=[
            pltpu.VMEM((8, 13, 8, 128), f32),
            pltpu.VMEM((8, 13, 8, 128), f32),
            pltpu.VMEM((8, 3, 8, 128), f32),
            pltpu.VMEM((8, 3, 8, 128), f32),
            pltpu.VMEM((BLOCKS * 32, 128), f32),
            pltpu.VMEM((BLOCKS + 1, 64, 128), f32),
            pltpu.VMEM((18, 9, 8, 128), f32),
            pltpu.VMEM((18, 9, 8, 128), f32),
            pltpu.VMEM((18, 24, 128), f32),
            pltpu.VMEM((2, 16, 128), jnp.int32),
            pltpu.VMEM((32, 128), jnp.int32),
            pltpu.VMEM((2, 16, 128), jnp.int32),
            pltpu.VMEM((2, 8, 128), jnp.int32),
            pltpu.VMEM((2, 2, 9, 8, 128), f32),
            pltpu.VMEM((2, 18, 8, 128), f32),
            pltpu.VMEM((4, 2, 8, 128), f32),
            pltpu.VMEM((BLOCKS * 32, 128), f32),
            dma((8,)),
            dma((8,)),
            dma((8,)),
            dma((8,)),
            dma((8,)),
            dma((8,)),
            dma((3,)),
            dma((3,)),
        ],
        compiler_params=pltpu.CompilerParams(collective_id=0, has_side_effects=True),
    )(
        following,
        first,
        column,
        lift,
        source,
        position,
        velocity,
        affine,
        deform,
        weighed,
        present,
        staying,
        boundary_mask.reshape(GX * GY, GZ),
    )


def solution(mesh):
    blocks = P(None, ("down", "cross"), None)
    flat = P(("down", "cross"))
    in_specs = (
        blocks,
        blocks,
        blocks,
        blocks,
        P(("down", "cross"), None),
        flat,
        flat,
        P("down", "cross", None),
        flat,
        flat,
    )
    step = functools.partial(body, mesh.shape["down"], mesh.shape["cross"])
    return jax.shard_map(step, mesh=mesh, in_specs=in_specs, out_specs=(blocks, blocks), check_vma=False)
```

time: 180 us -> 91.2 us (0.51)
  the two profiles are of different devices: /device:TPU:21 before, /device:TPU:1 now
where the time goes in v1:
time: 91.2 us; the launch traced here: 91.1 us
  Pallas kernels  80.3 us (88%)
  local copies, waits for them, and re-layouts  6.93 us (8%)
  other arithmetic  3.11 us (3%)
    pallas_call x1, Pallas kernels, body(): pl.pallas_call(functools.partial(kernel, n_down, n_cross), out_shape=(jax...  80.3 us
    unnamed x16, local copies, waits for them, and re-layouts  5.57 us

profile of v1, /device:TPU:1, one launch (start us, length us, event | category | flops | bytes accessed | tf_op | source)
XLA Modules:
  0.0 91.1 jit_solution(5661606275404692208)
XLA Ops:
  0.6 0.0 copy-start.3
  0.6 0.6 copy-done.3
  1.3 0.2 convert_reduce_fusion
  1.5 0.0 copy-start.5
  1.5 0.6 copy-done.5
  2.1 0.1 fusion.4
  2.2 0.0 copy-start.6
  2.2 0.6 copy-done.6
  2.9 0.5 fusion.7
  3.4 0.0 copy-start.2
  3.4 0.6 copy-done.2
  4.0 0.7 select_reduce_fusion.1
  4.7 0.2 fusion.5
  4.9 0.7 select_reduce_fusion.source_ref
  5.6 0.0 copy-start.1
  5.6 0.7 broadcast_in_dim.24.present_ref
  6.3 0.0 copy-start.4
  6.3 0.7 broadcast_in_dim.25.stay_ref
  7.0 0.0 copy-done.1
  7.0 0.0 copy-done.4
  7.0 0.7 fusion.2.mass_ref
  7.7 80.3 %shard_map.113 = (f32[24,64,128]{2,1,0:T(8,128)}, f32[25,64,128]{2,1,0:T(8,128)}) custom-call(s32[64]{0:T(128)} %get-tuple-element.3.next_ref, s32[64]{0:T(128)} %get-tuple-element.2.first_ref, s32[64]{0:T(128)} %copy-done.2, s32[64]{0:T(128)} %get-tuple-element.4.lift_ref, s32[64]{0:T(128)} %select_reduce_fusion.source_ref, f32[3,64,128]{2,1,0:T(8,128)} %pos_ref.1, ...), custom_call_target="tpu_custom_call" | custom-call | tf_op jit(solution)/shard_map/pallas_call | solution.py:560
  88.0 0.0 copy-start
  88.0 2.2 %copy.14 = f32[24,64,128]{2,1,0:T(8,128)} copy(f32[24,64,128]{2,1,0:T(8,128)} %get-tuple-element.10) | data formatting | bytes 1572864
  90.2 0.0 copy-done
  90.2 0.9 copy.15
  (4 shorter events, 0.0 us)
Async XLA Ops:
  0.6 0.7 copy-start.3
  1.5 0.7 copy-start.5
  2.2 0.7 copy-start.6
  3.4 0.6 copy-start.2
  5.6 1.4 %copy-start.1 = (f32[64,128]{1,0:T(8,128)S(1)}, f32[64,128]{1,0:T(8,128)}, u32[]{:S(2)}) copy-start(f32[64,128]{1,0:T(8,128)} %param.14) | copy-start | bytes 98308
  6.3 0.7 copy-start.4
  88.0 2.2 %copy-start = (f32[25,64,128]{2,1,0:T(8,128)S(1)}, f32[25,64,128]{2,1,0:T(8,128)}, u32[]{:S(2)}) copy-start(f32[25,64,128]{2,1,0:T(8,128)} %get-tuple-element.11) | copy-start | bytes 2457604

commit v2 on v1

--- a/solution.py
+++ b/solution.py
@@ -24,7 +24,9 @@
 mass_floor = 1.0
 move_list = ((-1, -1), (-1, 0), (-1, 1), (0, -1), (0, 1), (1, -1), (1, 0), (1, 1))
 early_order = (0, 2, 5, 7, 3, 4, 1, 6)
-early_first = 4
+early_first = 8
+p2g_batch = 4
+g2p_batch = 4
 
 MESH = pl.DeviceIdType.MESH
 f32 = jnp.float32
@@ -129,21 +131,60 @@
     return x + v + c + f
 
 
+def build_tables(count_ref, brick_ref, leave_ref, dest_ref, weight_ref, mass_ref, stay_ref, staged):
+    shape = (128, 128)
+    down = lax.broadcasted_iota(jnp.int32, shape, 0)
+    across = lax.broadcasted_iota(jnp.int32, shape, 1)
+
+    def padded(row, filler):
+        return jnp.concatenate([row, jnp.full((1, 128 - BLOCKS), filler, jnp.int32)], axis=1)
+
+    def upright(row):
+        return jnp.transpose(jnp.broadcast_to(row, shape))
+
+    def least(value):
+        return jnp.min(value, axis=0, keepdims=True)
+
+    count = upright(padded(count_ref[...], 0))[:BLOCKS]
+    lane = across[:BLOCKS]
+    mass_ref[...] = jnp.where(lane < count, weight_ref[...], 0.0)
+    brick = padded(brick_ref[...], 0)
+    column = brick >> 5
+    sides = upright(column)[:BLOCKS]
+    ids = down[:BLOCKS]
+    staged[0:1, :] = least(jnp.where((sides == column) & (ids > lane), ids, BLOCKS))
+    cell = ((sides >> 3) + 1) * 10 + (sides & 7) + 1
+    staged[1:2, :] = least(jnp.where(cell == lane, ids, BLOCKS))
+    staged[2:3, :] = column
+    staged[3:4, :] = (brick & 31) * 4
+    leave = padded(leave_ref[...], 0)
+    dest = padded(dest_ref[...], 4)
+    dest_up = upright(dest)[:BLOCKS]
+    leave_up = upright(leave)[:BLOCKS]
+    rank = jnp.sum(jnp.where((dest_up == dest) & (ids < lane), 1, 0), axis=0, keepdims=True)
+    move = jnp.where(dest > 4, dest - 1, dest)
+    slot = jnp.where(dest == 4, -1, move * 8 + rank)
+    slot_up = upright(slot)[:BLOCKS]
+    match = slot_up == lane
+    staged[4:5, :] = jnp.sum(jnp.where(match, leave_up, 0), axis=0, keepdims=True)
+    staged[5:6, :] = jnp.sum(jnp.where(match, 1, 0), axis=0, keepdims=True)
+    staged[6:8, :] = jnp.zeros((2, 128), jnp.int32)
+    gone = jnp.where((leave == ids) & (dest != 4), 1.0, 0.0)
+    stay_ref[...] = jnp.broadcast_to(1.0 - jnp.max(gone, axis=1, keepdims=True), (BLOCKS, SLOTS))
+
+
 def kernel(
     n_down,
     n_cross,
-    next_ref,
-    first_ref,
-    column_ref,
-    lift_ref,
-    source_ref,
+    count_ref,
+    brick_ref,
+    leave_ref,
+    dest_ref,
     pos_ref,
     vel_ref,
     aff_ref,
     def_ref,
-    mass_ref,
-    present_ref,
-    stay_ref,
+    weight_ref,
     mask_ref,
     state_ref,
     arrive_ref,
@@ -164,6 +205,11 @@
     face_y,
     corner,
     sums,
+    mass_ref,
+    stay_ref,
+    staged,
+    scalars,
+    scalar_sem,
     early_send,
     early_recv,
     late_send,
@@ -192,20 +238,29 @@
     for a, b in move_list:
         pl.semaphore_signal(barrier, inc=1, device_id=device(a, b), device_id_type=MESH)
 
-    for move in range(8):
-
-        def pick(k, carry, move=move):
-            source = source_ref[move * 8 + k]
-            early[move, 0:3, pl.ds(k, 1), :] = pos_ref[:, pl.ds(source, 1), :]
-            early[move, 3:12, pl.ds(k, 1), :] = def_ref[:, pl.ds(source, 1), :]
-            early[move, 12, pl.ds(k, 1), :] = (
-                mass_ref[pl.ds(source, 1), :] * present_ref[pl.ds(move * 8 + k, 1), :]
-            )
-            return carry
-
-        lax.fori_loop(0, 8, pick, 0)
+    build_tables(count_ref, brick_ref, leave_ref, dest_ref, weight_ref, mass_ref, stay_ref, staged)
+    to_scalars = pltpu.make_async_copy(staged, scalars, scalar_sem)
+    to_scalars.start()
     for par in range(2):
         mask_y[par] = mask_ref[pl.ds(par, 16, stride=16), :]
+    to_scalars.wait()
+    following = lambda b: scalars[0, b]
+    first_of = lambda cell: scalars[1, cell]
+    column_of = lambda b: scalars[2, b]
+    lift_of = lambda b: scalars[3, b]
+    source_of = lambda slot: scalars[4, slot]
+    present_of = lambda slot: scalars[5, slot]
+
+    def pick(move, carry):
+        for k in range(8):
+            source = source_of(move * 8 + k)
+            early[move, 0:3, k : k + 1, :] = pos_ref[:, pl.ds(source, 1), :]
+            early[move, 3:12, k : k + 1, :] = def_ref[:, pl.ds(source, 1), :]
+            here = present_of(move * 8 + k).astype(f32)
+            early[move, 12, k : k + 1, :] = mass_ref[pl.ds(source, 1), :] * here
+        return carry
+
+    lax.fori_loop(0, 8, pick, 0)
 
     def remote(source, target, send, recv, a, b):
         return pltpu.make_async_remote_copy(
@@ -256,9 +311,8 @@
 
     chain[BLOCKS] = jnp.zeros((64, 128), f32)
 
-    def to_bricks(step, carry):
-        b = (BLOCKS - 1) - step
-        lift = lift_ref[b]
+    def brick_sums(b):
+        lift = lift_of(b)
         x0 = pos_ref[0, pl.ds(b, 1), :]
         x1 = pos_ref[1, pl.ds(b, 1), :]
         x2 = pos_ref[2, pl.ds(b, 1), :]
@@ -286,32 +340,38 @@
         contract = (((1,), (1,)), ((), ()))
         found = lax.dot_general(lhs_high, stacked, contract, preferred_element_type=f32)
         found = found + lax.dot_general(lhs_low, stacked, contract, preferred_element_type=f32)
+        return lift, found
+
+    def placed(lift, found):
         wide = jnp.concatenate([found, jnp.zeros((64, 112), f32)], axis=1)
         folded = pltpu.roll(wide, lift, 1) + pltpu.roll(wide, (lift + 120) & 127, 1)
         lane = lane_iota(64)
-        here = (lane >= lift) & (lane < lift + 8)
-        chain[b] = jnp.where(here, folded, 0.0) + chain[next_ref[b]]
-        return carry
-
-    lax.fori_loop(0, BLOCKS, to_bricks, 0)
-
-    def clear(x, carry):
-        grid[x] = jnp.zeros((9, 8, 128), f32)
-        return carry
-
-    lax.fori_loop(0, 18, clear, 0)
-
-    def spread(column, carry):
-        p = column // NBY
-        q = lax.rem(column, NBY)
-        first = first_ref[column]
-        for x in range(4):
-            for yp in range(2):
-                start = 8 * (2 * x + yp)
-                grid[2 * p + x, q + yp] += chain[first, start : start + 8, :]
-        return carry
-
-    lax.fori_loop(0, NBX * NBY, spread, 0)
+        return jnp.where((lane >= lift) & (lane < lift + 8), folded, 0.0)
+
+    def to_bricks(step, carry):
+        blocks = [(BLOCKS - 1) - (step * p2g_batch + u) for u in range(p2g_batch)]
+        sums_of = [brick_sums(b) for b in blocks]
+        out = [placed(*found) for found in sums_of]
+        for b, value in zip(blocks, out):
+            chain[b] = value + chain[following(b)]
+        return carry
+
+    lax.fori_loop(0, BLOCKS // p2g_batch, to_bricks, 0)
+
+    def spread(p, carry):
+        for q in range(9):
+            cells = [[first_of((p + 1 - dp) * 10 + (q + 1 - dq)) for dq in range(2)] for dp in range(2)]
+            for x in range(2):
+                total = None
+                for dp in range(2):
+                    for dq in range(2):
+                        start = 8 * (2 * (x + 2 * dp) + dq)
+                        value = chain[cells[dp][dq], start : start + 8, :]
+                        total = value if total is None else total + value
+                grid[2 * p + x, q] = total
+        return carry
+
+    lax.fori_loop(0, 9, spread, 0)
 
     halo_copies = []
     faces = {-1: 0, 1: 1}
@@ -407,30 +467,26 @@
     lane8 = lane_iota(8)
 
     def brick_tiles(b):
-        column = column_ref[b]
+        column = column_of(b)
         p = column // NBY
         q = lax.rem(column, NBY)
         return [node_v[2 * p + x, q + yp] for x in range(4) for yp in range(2)]
 
     for move in range(8):
 
-        def window(k, carry, move=move):
-            b = source_ref[move * 8 + k]
-            lift = lift_ref[b]
+        packed = [jnp.zeros((8, 128), f32)] * 4
+        for k in range(8):
+            b = source_of(move * 8 + k)
+            lift = lift_of(b)
             tiles = brick_tiles(b)
-            shift = (8 * k - lift + 128) & 127
+            shift = (8 * k + 128 - lift) & 127
             local = lane8 - 8 * k
             low = (local >= 0) & (local < 8) & (local + lift < GZ)
             local = local - 64
             high = (local >= 0) & (local < 8) & (local + lift < GZ)
-            out = []
             for t in range(4):
-                kept = jnp.where(low, pltpu.roll(tiles[t], shift, 1), carry[t])
-                out.append(jnp.where(high, pltpu.roll(tiles[t + 4], (shift + 64) & 127, 1), kept))
-            return tuple(out)
-
-        zero = jnp.zeros((8, 128), f32)
-        packed = lax.fori_loop(0, 8, window, (zero,) * 4)
+                kept = jnp.where(low, pltpu.roll(tiles[t], shift, 1), packed[t])
+                packed[t] = jnp.where(high, pltpu.roll(tiles[t + 4], (shift + 64) & 127, 1), kept)
         for t in range(3):
             moved = pltpu.roll(packed[3], (8 - (2 + 2 * t)) & 7, 0)
             late[move, t] = jnp.where(row8 < 2, moved, packed[t])
@@ -449,20 +505,26 @@
         for t in range(4):
             sums[pl.ds(base + 8 * t, 8), :] = total[t]
 
-    def resident(b, carry):
-        lift = lift_ref[b]
-        stack = jnp.concatenate(brick_tiles(b), axis=0)
-        total = gathered(
-            windows(stack, 128 - lift),
-            pos_ref[0, pl.ds(b, 1), :],
-            pos_ref[1, pl.ds(b, 1), :],
-            pos_ref[2, pl.ds(b, 1), :],
-            GZ - lift,
-        )
-        put_sums(b, total)
-        return carry
-
-    lax.fori_loop(0, BLOCKS, resident, 0)
+    def resident(step, carry):
+        blocks = [step * g2p_batch + u for u in range(g2p_batch)]
+        totals = []
+        for b in blocks:
+            lift = lift_of(b)
+            stack = jnp.concatenate(brick_tiles(b), axis=0)
+            totals.append(
+                gathered(
+                    windows(stack, 128 - lift),
+                    pos_ref[0, pl.ds(b, 1), :],
+                    pos_ref[1, pl.ds(b, 1), :],
+                    pos_ref[2, pl.ds(b, 1), :],
+                    GZ - lift,
+                )
+            )
+        for b, total in zip(blocks, totals):
+            put_sums(b, total)
+        return carry
+
+    lax.fori_loop(0, BLOCKS // g2p_batch, resident, 0)
 
     def finish(g, carry):
         rows = pl.ds(pl.multiple_of(g * 8, 8), 8)
@@ -486,18 +548,23 @@
         low_stack = jnp.concatenate(packed, axis=0)
         stack = jnp.concatenate([low_stack, pltpu.roll(low_stack, 64, 1)], axis=0)
 
-        def arriving(k, carry, move=move, stack=stack):
-            total = gathered(
-                windows(stack, 128 - 8 * k),
-                early_in[move, 0, pl.ds(k, 1), :],
-                early_in[move, 1, pl.ds(k, 1), :],
-                early_in[move, 2, pl.ds(k, 1), :],
-                None,
-            )
-            put_sums(k, total)
+        def arriving(step, carry, move=move, stack=stack):
+            ks = [step * g2p_batch + u for u in range(g2p_batch)]
+            totals = [
+                gathered(
+                    windows(stack, 128 - 8 * k),
+                    early_in[move, 0, pl.ds(k, 1), :],
+                    early_in[move, 1, pl.ds(k, 1), :],
+                    early_in[move, 2, pl.ds(k, 1), :],
+                    None,
+                )
+                for k in ks
+            ]
+            for k, total in zip(ks, totals):
+                put_sums(k, total)
             return carry
 
-        lax.fori_loop(0, 8, arriving, 0)
+        lax.fori_loop(0, 8 // g2p_batch, arriving, 0)
         rows = pl.ds(move * 8, 8)
         position = [early_in[move, c] for c in range(3)]
         deform = [early_in[move, 3 + c] for c in range(9)]
@@ -506,31 +573,6 @@
         for row, value in enumerate(final_rows(sums, 0, position, deform)):
             arrive_ref[row, rows, :] = value * keep
         arrive_ref[24, rows, :] = mass
-
-
-def brick_tables(block_brick):
-    column = block_brick // 32
-    ids = jnp.arange(BLOCKS, dtype=jnp.int32)
-    later = (column[:, None] == column[None, :]) & (ids[None, :] > ids[:, None])
-    following = jnp.min(jnp.where(later, ids[None, :], BLOCKS), axis=1)
-    held = column[None, :] == jnp.arange(NBX * NBY, dtype=jnp.int32)[:, None]
-    first = jnp.min(jnp.where(held, ids[None, :], BLOCKS), axis=1)
-    return following, first, column, (block_brick % 32) * 4
-
-
-def leaving_tables(leaving_block, leaving_dest):
-    order = jnp.arange(BLOCKS, dtype=jnp.int32)
-    ahead = (leaving_dest[:, None] == leaving_dest[None, :]) & (order[None, :] < order[:, None])
-    entry_rank = jnp.sum(ahead.astype(jnp.int32), axis=1)
-    slot_index = jnp.arange(8 * MIG, dtype=jnp.int32)
-    move_index = slot_index // MIG
-    wanted = move_index + (move_index >= 4).astype(jnp.int32)
-    matches = (leaving_dest[None, :] == wanted[:, None]) & (entry_rank[None, :] == (slot_index % MIG)[:, None])
-    source = jnp.sum(matches.astype(jnp.int32) * leaving_block[None, :], axis=1)
-    present = jnp.any(matches, axis=1).astype(f32)
-    hit_table = (leaving_block[:, None] == order[None, :]) & (leaving_dest[:, None] != 4)
-    staying = 1.0 - jnp.any(hit_table, axis=0).astype(f32)
-    return source, present, staying
 
 
 def body(
@@ -547,14 +589,6 @@
     leaving_block,
     leaving_dest,
 ):
-    slot_index = lax.broadcasted_iota(jnp.int32, particle_mass.shape, 1)
-    weighed = jnp.where(slot_index < block_count[:, None], particle_mass, 0.0)
-    following, first, column, lift = brick_tables(block_brick)
-    source, present, staying = leaving_tables(leaving_block, leaving_dest)
-    wide = (BLOCKS, SLOTS)
-    present = jnp.broadcast_to(present[:, None], wide)
-    staying = jnp.broadcast_to(staying[:, None], wide)
-    smem = pl.BlockSpec(memory_space=pltpu.SMEM)
     vmem = pl.BlockSpec(memory_space=pltpu.VMEM)
     dma = pltpu.SemaphoreType.DMA
     return pl.pallas_call(
@@ -563,7 +597,7 @@
             jax.ShapeDtypeStruct((24, BLOCKS, SLOTS), f32),
             jax.ShapeDtypeStruct((25, BLOCKS, SLOTS), f32),
         ),
-        in_specs=[smem] * 5 + [vmem] * 8,
+        in_specs=[vmem] * 10,
         out_specs=(vmem, vmem),
         scratch_shapes=[
             pltpu.VMEM((8, 13, 8, 128), f32),
@@ -583,6 +617,11 @@
             pltpu.VMEM((2, 18, 8, 128), f32),
             pltpu.VMEM((4, 2, 8, 128), f32),
             pltpu.VMEM((BLOCKS * 32, 128), f32),
+            pltpu.VMEM((BLOCKS, SLOTS), f32),
+            pltpu.VMEM((BLOCKS, SLOTS), f32),
+            pltpu.VMEM((8, 128), jnp.int32),
+            pltpu.SMEM((8, 128), jnp.int32),
+            dma,
             dma((8,)),
             dma((8,)),
             dma((8,)),
@@ -594,18 +633,15 @@
         ],
         compiler_params=pltpu.CompilerParams(collective_id=0, has_side_effects=True),
     )(
-        following,
-        first,
-        column,
-        lift,
-        source,
+        block_count.reshape(1, BLOCKS),
+        block_brick.reshape(1, BLOCKS),
+        leaving_block.reshape(1, BLOCKS),
+        leaving_dest.reshape(1, BLOCKS),
         position,
         velocity,
         affine,
         deform,
-        weighed,
-        present,
-        staying,
+        particle_mass,
         boundary_mask.reshape(GX * GY, GZ),
     )
 

time: 91.2 us -> 55.7 us (0.61)
  Pallas kernels: 80.3 us -> 51.9 us
  local copies, waits for them, and re-layouts: 6.93 us -> 3.06 us
  other arithmetic: 3.11 us -> 0 us
    pallas_call x1, Pallas kernels: 80.3 us -> 51.9 us  [body(): pl.pallas_call(functools.partial(kernel, n_down, n_cross), out_shape=(jax...]
    unnamed x16 -> x4, local copies, waits for them, and re-layouts: 5.57 us -> 3.06 us
    broadcast_in_dim x2 -> x0, local copies, waits for them, and re-layouts: 1.36 us -> none  [the longest x1 0.69 us: body(): present = jnp.broadcast_to(present[:, None], wide)]
where the time goes in v2:
time: 55.7 us; the launch traced here: 55.6 us
  Pallas kernels  51.9 us (93%)
  local copies, waits for them, and re-layouts  3.06 us (5%)
  between operations  0.65 us (1%)
    pallas_call x1, Pallas kernels, body(): pl.pallas_call(functools.partial(kernel, n_down, n_cross), out_shape=(jax...  51.9 us
    unnamed x4, local copies, waits for them, and re-layouts  3.06 us

profile of v2, /device:TPU:1, one launch (start us, length us, event | category | flops | bytes accessed | tf_op | source)
XLA Modules:
  0.0 55.6 jit_solution(13873588690094304208)
XLA Ops:
  0.6 51.9 %shard_map.113 = (f32[24,64,128]{2,1,0:T(8,128)}, f32[25,64,128]{2,1,0:T(8,128)}) custom-call(s32[1,64]{1,0:T(1,128)} %bitcast.6, s32[1,64]{1,0:T(1,128)} %bitcast.7, s32[1,64]{1,0:T(1,128)} %bitcast.8, s32[1,64]{1,0:T(1,128)} %bitcast.9, f32[3,64,128]{2,1,0:T(8,128)} %pos_ref.1, f32[3,64,128]{2,1,0:T(8,128)} %vel_ref.1, f32[9,64,128]{2,1,0:T(8,128)} %aff_ref.1, ...), custom_call_target="tpu_custom_call" | custom-call | tf_op jit(solution)/shard_map/pallas_call | solution.py:594
  52.5 0.0 copy-start
  52.5 2.2 %copy.14 = f32[24,64,128]{2,1,0:T(8,128)} copy(f32[24,64,128]{2,1,0:T(8,128)} %get-tuple-element.4) | data formatting | bytes 1572864
  54.7 0.0 copy-done
  54.7 0.9 %copy.15 = f32[25,64,128]{2,1,0:T(8,128)} copy(f32[25,64,128]{2,1,0:T(8,128)S(1)} %copy-done) | data formatting | bytes 1638400
Async XLA Ops:
  52.5 2.2 %copy-start = (f32[25,64,128]{2,1,0:T(8,128)S(1)}, f32[25,64,128]{2,1,0:T(8,128)}, u32[]{:S(2)}) copy-start(f32[25,64,128]{2,1,0:T(8,128)} %get-tuple-element.5) | copy-start | bytes 2457604

commit v3 on v2

--- a/solution.py
+++ b/solution.py
@@ -24,9 +24,10 @@
 mass_floor = 1.0
 move_list = ((-1, -1), (-1, 0), (-1, 1), (0, -1), (0, 1), (1, -1), (1, 0), (1, 1))
 early_order = (0, 2, 5, 7, 3, 4, 1, 6)
-early_first = 8
-p2g_batch = 4
-g2p_batch = 4
+arrival_order = (1, 6, 0, 2, 5, 7, 3, 4)
+early_first = 4
+p2g_batch = 8
+g2p_batch = 8
 
 MESH = pl.DeviceIdType.MESH
 f32 = jnp.float32
@@ -180,14 +181,24 @@
     brick_ref,
     leave_ref,
     dest_ref,
+    pos_hbm,
+    vel_hbm,
+    aff_hbm,
+    def_hbm,
+    weight_hbm,
+    mask_hbm,
+    state_out,
+    arrive_out,
     pos_ref,
     vel_ref,
     aff_ref,
     def_ref,
     weight_ref,
     mask_ref,
+    load_sem,
     state_ref,
     arrive_ref,
+    out_sem,
     early,
     early_in,
     late,
@@ -219,6 +230,21 @@
     mask_send,
     mask_recv,
 ):
+    loads = [
+        pltpu.make_async_copy(source, target, load_sem.at[n])
+        for n, (source, target) in enumerate(
+            (
+                (weight_hbm, weight_ref),
+                (mask_hbm, mask_ref),
+                (pos_hbm, pos_ref),
+                (def_hbm, def_ref),
+                (vel_hbm, vel_ref),
+                (aff_hbm, aff_ref),
+            )
+        )
+    ]
+    for load in loads:
+        load.start()
     i = lax.axis_index("down")
     j = lax.axis_index("cross")
 
@@ -232,18 +258,55 @@
         if b:
             other = (j + b >= 0) & (j + b < n_cross)
             valid = other if valid is None else valid & other
-        return valid.astype(f32)
+        return valid
+
+    class Edge:
+        def __init__(self, copy, a, b):
+            self.copy, self.a, self.b = copy, a, b
+
+        def start(self):
+            pl.when(inside(self.a, self.b))(self.copy.start)
+
+        def wait_send(self):
+            pl.when(inside(self.a, self.b))(self.copy.wait_send)
+
+        def wait_recv(self):
+            pl.when(inside(-self.a, -self.b))(self.copy.wait_recv)
 
     barrier = pltpu.get_barrier_semaphore()
+    neighbours = 0
     for a, b in move_list:
-        pl.semaphore_signal(barrier, inc=1, device_id=device(a, b), device_id_type=MESH)
-
+
+        @pl.when(inside(a, b))
+        def greet(a=a, b=b):
+            pl.semaphore_signal(barrier, inc=1, device_id=device(a, b), device_id_type=MESH)
+
+        neighbours = neighbours + inside(a, b).astype(jnp.int32)
+
+    def fill(target, a, b):
+        @pl.when(jnp.logical_not(inside(a, b)))
+        def zeros():
+            target[...] = jnp.zeros(target.shape, target.dtype)
+
+    for sign in (-1, 1):
+        fill(face_x.at[(sign + 1) // 2], -sign, 0)
+        fill(face_y.at[(sign + 1) // 2], 0, -sign)
+        for other in (-1, 1):
+            fill(corner.at[sign + 1 + (other + 1) // 2], -sign, -other)
+    fill(mask_x_in, 1, 0)
+    fill(mask_y_in, 0, 1)
+    fill(mask_c_in, 1, 1)
+
+    loads[0].wait()
     build_tables(count_ref, brick_ref, leave_ref, dest_ref, weight_ref, mass_ref, stay_ref, staged)
     to_scalars = pltpu.make_async_copy(staged, scalars, scalar_sem)
     to_scalars.start()
+    loads[1].wait()
     for par in range(2):
         mask_y[par] = mask_ref[pl.ds(par, 16, stride=16), :]
     to_scalars.wait()
+    loads[2].wait()
+    loads[3].wait()
     following = lambda b: scalars[0, b]
     first_of = lambda cell: scalars[1, cell]
     column_of = lambda b: scalars[2, b]
@@ -263,7 +326,7 @@
     lax.fori_loop(0, 8, pick, 0)
 
     def remote(source, target, send, recv, a, b):
-        return pltpu.make_async_remote_copy(
+        copy = pltpu.make_async_remote_copy(
             src_ref=source,
             dst_ref=target,
             send_sem=send,
@@ -271,6 +334,7 @@
             device_id=device(a, b),
             device_id_type=MESH,
         )
+        return Edge(copy, a, b)
 
     early_copies = [
         remote(early.at[m], early_in.at[m], early_send.at[m], early_recv.at[m], a, b)
@@ -286,12 +350,6 @@
         remote(mask_y.at[:, pl.ds(0, 8)], mask_c_in, mask_send.at[2], mask_recv.at[2], -1, -1),
     ]
 
-    pl.semaphore_wait(barrier, 8)
-    for copy in mask_copies:
-        copy.start()
-    for m in early_order[:early_first]:
-        early_copies[m].start()
-
     def terms(g, carry):
         rows = pl.ds(pl.multiple_of(g * 8, 8), 8)
         deform = [def_ref[c, rows, :] for c in range(9)]
@@ -307,7 +365,15 @@
                     table[pl.ds(row, 8, stride=32), :] = value
         return carry
 
+    loads[4].wait()
+    loads[5].wait()
     lax.fori_loop(0, 8, terms, 0)
+
+    pl.semaphore_wait(barrier, neighbours)
+    for copy in mask_copies:
+        copy.start()
+    for m in early_order[:early_first]:
+        early_copies[m].start()
 
     chain[BLOCKS] = jnp.zeros((64, 128), f32)
 
@@ -416,10 +482,10 @@
 
     lax.fori_loop(2, 16, interior, 0)
     for copy in mask_copies:
-        copy.wait()
-    past_x = inside(1, 0)
-    past_y = inside(0, 1)
-    past_c = inside(1, 1)
+        copy.wait_recv()
+    past_x = inside(1, 0).astype(f32)
+    past_y = inside(0, 1).astype(f32)
+    past_c = inside(1, 1).astype(f32)
     for xx in range(2):
         movable[16 + xx, 0:16, :] = (1 - mask_x_in[pl.ds(16 * xx, 16), :]).astype(f32) * past_x
         for par in range(2):
@@ -434,14 +500,13 @@
 
     lax.fori_loop(0, 16, side_mask, 0)
     for copy in halo_copies:
-        copy.wait()
-    has = {(a, b): inside(-a, -b) for a, b in move_list}
+        copy.wait_recv()
 
     def low_high(yp):
         for a in (-1, 1):
             for xx in range(2):
                 x = xx if a == 1 else 16 + xx
-                yield a, xx, x, grid[x, yp] + face_x[faces[a], xx, yp] * has[(a, 0)]
+                yield a, xx, x, grid[x, yp] + face_x[faces[a], xx, yp]
 
     def edge_x(yp, carry):
         for _, _, x, tile in low_high(yp):
@@ -453,15 +518,15 @@
     def edge_y(x, carry):
         for b in (-1, 1):
             yp = 0 if b == 1 else 8
-            put_velocity(x, yp, grid[x, yp] + face_y[faces[b], x] * has[(0, b)])
+            put_velocity(x, yp, grid[x, yp] + face_y[faces[b], x])
         return carry
 
     lax.fori_loop(2, 16, edge_y, 0)
     for b in (-1, 1):
         yp = 0 if b == 1 else 8
         for a, xx, x, tile in low_high(yp):
-            tile = tile + face_y[faces[b], x] * has[(0, b)]
-            tile = tile + corner[2 * faces[a] + faces[b], xx] * has[(a, b)]
+            tile = tile + face_y[faces[b], x]
+            tile = tile + corner[2 * faces[a] + faces[b], xx]
             put_velocity(x, yp, tile)
 
     lane8 = lane_iota(8)
@@ -472,8 +537,7 @@
         q = lax.rem(column, NBY)
         return [node_v[2 * p + x, q + yp] for x in range(4) for yp in range(2)]
 
-    for move in range(8):
-
+    for move in early_order:
         packed = [jnp.zeros((8, 128), f32)] * 4
         for k in range(8):
             b = source_of(move * 8 + k)
@@ -536,43 +600,75 @@
         return carry
 
     lax.fori_loop(0, 8, finish, 0)
-
-    for move, (a, b) in enumerate(move_list):
-        early_copies[move].wait()
-        late_copies[move].wait()
-        packed = [late_in[move, t] for t in range(3)]
-        last = jnp.zeros((8, 128), f32)
-        for t in range(3):
-            last = last + pltpu.roll(jnp.where(row8 < 2, packed[t], 0.0), 2 + 2 * t, 0)
-        packed.append(last)
-        low_stack = jnp.concatenate(packed, axis=0)
-        stack = jnp.concatenate([low_stack, pltpu.roll(low_stack, 64, 1)], axis=0)
-
-        def arriving(step, carry, move=move, stack=stack):
-            ks = [step * g2p_batch + u for u in range(g2p_batch)]
-            totals = [
-                gathered(
-                    windows(stack, 128 - 8 * k),
-                    early_in[move, 0, pl.ds(k, 1), :],
-                    early_in[move, 1, pl.ds(k, 1), :],
-                    early_in[move, 2, pl.ds(k, 1), :],
-                    None,
-                )
-                for k in ks
-            ]
-            for k, total in zip(ks, totals):
-                put_sums(k, total)
-            return carry
-
-        lax.fori_loop(0, 8 // g2p_batch, arriving, 0)
+    stores = [pltpu.make_async_copy(state_ref, state_out, out_sem.at[8])]
+    stores[0].start()
+
+    for move in arrival_order:
+        a, b = move_list[move]
+        early_copies[move].wait_recv()
+        late_copies[move].wait_recv()
         rows = pl.ds(move * 8, 8)
-        position = [early_in[move, c] for c in range(3)]
-        deform = [early_in[move, 3 + c] for c in range(9)]
-        mass = early_in[move, 12] * inside(-a, -b)
-        keep = jnp.where(mass > 0.0, 1.0, 0.0)
-        for row, value in enumerate(final_rows(sums, 0, position, deform)):
-            arrive_ref[row, rows, :] = value * keep
-        arrive_ref[24, rows, :] = mass
+
+        @pl.when(jnp.logical_not(inside(-a, -b)))
+        def nobody(rows=rows):
+            arrive_ref[:, rows, :] = jnp.zeros((25, 8, 128), f32)
+
+        @pl.when(inside(-a, -b))
+        def somebody(move=move, rows=rows):
+            packed = [late_in[move, t] for t in range(3)]
+            last = jnp.zeros((8, 128), f32)
+            for t in range(3):
+                last = last + pltpu.roll(jnp.where(row8 < 2, packed[t], 0.0), 2 + 2 * t, 0)
+            packed.append(last)
+            low_stack = jnp.concatenate(packed, axis=0)
+            stack = jnp.concatenate([low_stack, pltpu.roll(low_stack, 64, 1)], axis=0)
+
+            def arriving(step, carry, move=move, stack=stack):
+                ks = [step * g2p_batch + u for u in range(g2p_batch)]
+                totals = [
+                    gathered(
+                        windows(stack, 128 - 8 * k),
+                        early_in[move, 0, pl.ds(k, 1), :],
+                        early_in[move, 1, pl.ds(k, 1), :],
+                        early_in[move, 2, pl.ds(k, 1), :],
+                        None,
+                    )
+                    for k in ks
+                ]
+                for k, total in zip(ks, totals):
+                    put_sums(k, total)
+                return carry
+
+            lax.fori_loop(0, 8 // g2p_batch, arriving, 0)
+            position = [early_in[move, c] for c in range(3)]
+            deform = [early_in[move, 3 + c] for c in range(9)]
+            mass = early_in[move, 12]
+            keep = jnp.where(mass > 0.0, 1.0, 0.0)
+            for row, value in enumerate(final_rows(sums, 0, position, deform)):
+                arrive_ref[row, rows, :] = value * keep
+            arrive_ref[24, rows, :] = mass
+
+        store = pltpu.make_async_copy(arrive_ref.at[:, rows], arrive_out.at[:, rows], out_sem.at[move])
+        store.start()
+        stores.append(store)
+    for copy in early_copies + late_copies + halo_copies + mask_copies:
+        copy.wait_send()
+    for store in stores:
+        store.wait()
+
+
+def pass_on(state, arrivals, state_out, arrive_out, held, held_too, in_sem, out_sem):
+    chunks = [(state, held, state_out, pl.ds(6 * n, 6)) for n in range(4)]
+    chunks += [(arrivals, held_too, arrive_out, pl.ds(5 * n, 5)) for n in range(5)]
+    taken = [pltpu.make_async_copy(a.at[d], v.at[d], in_sem.at[n]) for n, (a, v, _, d) in enumerate(chunks)]
+    given = [pltpu.make_async_copy(v.at[d], o.at[d], out_sem.at[n]) for n, (_, v, o, d) in enumerate(chunks)]
+    for copy in taken:
+        copy.start()
+    for copy, onward in zip(taken, given):
+        copy.wait()
+        onward.start()
+    for onward in given:
+        onward.wait()
 
 
 def body(
@@ -591,15 +687,26 @@
 ):
     vmem = pl.BlockSpec(memory_space=pltpu.VMEM)
     dma = pltpu.SemaphoreType.DMA
-    return pl.pallas_call(
+    hbm = pl.BlockSpec(memory_space=pltpu.HBM)
+    results = pl.pallas_call(
         functools.partial(kernel, n_down, n_cross),
         out_shape=(
             jax.ShapeDtypeStruct((24, BLOCKS, SLOTS), f32),
             jax.ShapeDtypeStruct((25, BLOCKS, SLOTS), f32),
         ),
-        in_specs=[vmem] * 10,
-        out_specs=(vmem, vmem),
+        in_specs=[vmem] * 4 + [pl.BlockSpec(memory_space=pltpu.HBM)] * 6,
+        out_specs=(hbm, hbm),
         scratch_shapes=[
+            pltpu.VMEM((3, BLOCKS, SLOTS), f32),
+            pltpu.VMEM((3, BLOCKS, SLOTS), f32),
+            pltpu.VMEM((9, BLOCKS, SLOTS), f32),
+            pltpu.VMEM((9, BLOCKS, SLOTS), f32),
+            pltpu.VMEM((BLOCKS, SLOTS), f32),
+            pltpu.VMEM((GX * GY, GZ), jnp.int32),
+            dma((6,)),
+            pltpu.VMEM((24, BLOCKS, SLOTS), f32),
+            pltpu.VMEM((25, BLOCKS, SLOTS), f32),
+            dma((9,)),
             pltpu.VMEM((8, 13, 8, 128), f32),
             pltpu.VMEM((8, 13, 8, 128), f32),
             pltpu.VMEM((8, 3, 8, 128), f32),
@@ -644,6 +751,21 @@
         particle_mass,
         boundary_mask.reshape(GX * GY, GZ),
     )
+    return pl.pallas_call(
+        pass_on,
+        out_shape=(
+            jax.ShapeDtypeStruct((24, BLOCKS, SLOTS), f32),
+            jax.ShapeDtypeStruct((25, BLOCKS, SLOTS), f32),
+        ),
+        in_specs=[hbm, hbm],
+        out_specs=(hbm, hbm),
+        scratch_shapes=[
+            pltpu.VMEM((24, BLOCKS, SLOTS), f32),
+            pltpu.VMEM((25, BLOCKS, SLOTS), f32),
+            dma((9,)),
+            dma((9,)),
+        ],
+    )(*results)
 
 
 def solution(mesh):

time: 55.7 us -> 47.2 us (0.85)
  the two profiles are of different devices: /device:TPU:1 before, /device:TPU:28 now
where the time goes in v3:
time: 47.2 us; the launch traced here: 47.1 us
  Pallas kernels  46.4 us (98%)
  between operations  0.64 us (1%)
    pallas_call x1, Pallas kernels, body(): pl.pallas_call(functools.partial(kernel, n_down, n_cross), out_shape=(jax...  44.1 us
    pallas_call x1, Pallas kernels, body(): pl.pallas_call(pass_on, out_shape=(jax.ShapeDtypeStruct((24, BLOCKS, SLOT...  2.32 us

profile of v3, /device:TPU:28, one launch (start us, length us, event | category | flops | bytes accessed | tf_op | source)
XLA Modules:
  0.0 47.1 jit_solution(3611092552575258569)
XLA Ops:
  0.6 44.1 %shard_map.113 = (f32[24,64,128]{2,1,0:T(8,128)}, f32[25,64,128]{2,1,0:T(8,128)}) custom-call(s32[1,64]{1,0:T(1,128)} %bitcast.6, s32[1,64]{1,0:T(1,128)} %bitcast.7, s32[1,64]{1,0:T(1,128)} %bitcast.8, s32[1,64]{1,0:T(1,128)} %bitcast.9, f32[3,64,128]{2,1,0:T(8,128)} %pos_hbm.1, f32[3,64,128]{2,1,0:T(8,128)} %vel_hbm.1, f32[9,64,128]{2,1,0:T(8,128)} %aff_hbm.1, ...), custom_call_target="tpu_custom_call" | custom-call | tf_op jit(solution)/shard_map/pallas_call | solution.py:691
  44.7 2.3 %shard_map.114 = (f32[24,64,128]{2,1,0:T(8,128)}, f32[25,64,128]{2,1,0:T(8,128)}) custom-call(f32[24,64,128]{2,1,0:T(8,128)} %get-tuple-element.4.state, f32[25,64,128]{2,1,0:T(8,128)} %get-tuple-element.5.arrivals), custom_call_target="tpu_custom_call" | custom-call | tf_op jit(solution)/shard_map/pallas_call | solution.py:754

commit v4 on v3

--- a/solution.py
+++ b/solution.py
@@ -350,6 +350,10 @@
         remote(mask_y.at[:, pl.ds(0, 8)], mask_c_in, mask_send.at[2], mask_recv.at[2], -1, -1),
     ]
 
+    pl.semaphore_wait(barrier, neighbours)
+    for m in early_order[:early_first]:
+        early_copies[m].start()
+
     def terms(g, carry):
         rows = pl.ds(pl.multiple_of(g * 8, 8), 8)
         deform = [def_ref[c, rows, :] for c in range(9)]
@@ -368,12 +372,6 @@
     loads[4].wait()
     loads[5].wait()
     lax.fori_loop(0, 8, terms, 0)
-
-    pl.semaphore_wait(barrier, neighbours)
-    for copy in mask_copies:
-        copy.start()
-    for m in early_order[:early_first]:
-        early_copies[m].start()
 
     chain[BLOCKS] = jnp.zeros((64, 128), f32)
 
@@ -434,7 +432,7 @@
                         start = 8 * (2 * (x + 2 * dp) + dq)
                         value = chain[cells[dp][dq], start : start + 8, :]
                         total = value if total is None else total + value
-                grid[2 * p + x, q] = total
+                grid[q, 2 * p + x] = total
         return carry
 
     lax.fori_loop(0, 9, spread, 0)
@@ -445,14 +443,16 @@
         xs = pl.ds(16, 2) if a == 1 else pl.ds(0, 2)
         y = 8 if b == 1 else 0
         if b == 0:
-            source, target = grid.at[xs], face_x.at[faces[a]]
+            source, target = grid.at[:, xs], face_x.at[faces[a]]
         elif a == 0:
-            source, target = grid.at[:, y], face_y.at[faces[b]]
+            source, target = grid.at[y], face_y.at[faces[b]]
         else:
-            source, target = grid.at[xs, y], corner.at[2 * faces[a] + faces[b]]
+            source, target = grid.at[y, xs], corner.at[2 * faces[a] + faces[b]]
         halo_copies.append(remote(source, target, halo_send.at[m], halo_recv.at[m], a, b))
     for m in (3, 4, 0, 2, 5, 7, 1, 6):
         halo_copies[m].start()
+    for copy in mask_copies:
+        copy.start()
     for m in early_order[early_first:]:
         early_copies[m].start()
 
@@ -477,7 +477,7 @@
 
     def interior(x, carry):
         for yp in range(1, 8):
-            put_velocity(x, yp, grid[x, yp])
+            put_velocity(x, yp, grid[yp, x])
         return carry
 
     lax.fori_loop(2, 16, interior, 0)
@@ -506,7 +506,7 @@
         for a in (-1, 1):
             for xx in range(2):
                 x = xx if a == 1 else 16 + xx
-                yield a, xx, x, grid[x, yp] + face_x[faces[a], xx, yp]
+                yield a, xx, x, grid[yp, x] + face_x[faces[a], yp, xx]
 
     def edge_x(yp, carry):
         for _, _, x, tile in low_high(yp):
@@ -518,7 +518,7 @@
     def edge_y(x, carry):
         for b in (-1, 1):
             yp = 0 if b == 1 else 8
-            put_velocity(x, yp, grid[x, yp] + face_y[faces[b], x])
+            put_velocity(x, yp, grid[yp, x] + face_y[faces[b], x])
         return carry
 
     lax.fori_loop(2, 16, edge_y, 0)
@@ -713,14 +713,14 @@
             pltpu.VMEM((8, 3, 8, 128), f32),
             pltpu.VMEM((BLOCKS * 32, 128), f32),
             pltpu.VMEM((BLOCKS + 1, 64, 128), f32),
-            pltpu.VMEM((18, 9, 8, 128), f32),
+            pltpu.VMEM((9, 18, 8, 128), f32),
             pltpu.VMEM((18, 9, 8, 128), f32),
             pltpu.VMEM((18, 24, 128), f32),
             pltpu.VMEM((2, 16, 128), jnp.int32),
             pltpu.VMEM((32, 128), jnp.int32),
             pltpu.VMEM((2, 16, 128), jnp.int32),
             pltpu.VMEM((2, 8, 128), jnp.int32),
-            pltpu.VMEM((2, 2, 9, 8, 128), f32),
+            pltpu.VMEM((2, 9, 2, 8, 128), f32),
             pltpu.VMEM((2, 18, 8, 128), f32),
             pltpu.VMEM((4, 2, 8, 128), f32),
             pltpu.VMEM((BLOCKS * 32, 128), f32),

time: 47.2 us -> 46.8 us (level)
  no operation moved by 1% of the time
where the time goes in v4:
time: 46.8 us; the launch traced here: 46.7 us
  Pallas kernels  46 us (98%)
  between operations  0.64 us (1%)
    pallas_call x1, Pallas kernels, body(): pl.pallas_call(functools.partial(kernel, n_down, n_cross), out_shape=(jax...  43.7 us
    pallas_call x1, Pallas kernels, body(): pl.pallas_call(pass_on, out_shape=(jax.ShapeDtypeStruct((24, BLOCKS, SLOT...  2.32 us

profile of v4, /device:TPU:28, one launch (start us, length us, event | category | flops | bytes accessed | tf_op | source)
XLA Modules:
  0.0 46.7 jit_solution(1080405030802937757)
XLA Ops:
  0.6 43.7 %shard_map.113 = (f32[24,64,128]{2,1,0:T(8,128)}, f32[25,64,128]{2,1,0:T(8,128)}) custom-call(s32[1,64]{1,0:T(1,128)} %bitcast.6, s32[1,64]{1,0:T(1,128)} %bitcast.7, s32[1,64]{1,0:T(1,128)} %bitcast.8, s32[1,64]{1,0:T(1,128)} %bitcast.9, f32[3,64,128]{2,1,0:T(8,128)} %pos_hbm.1, f32[3,64,128]{2,1,0:T(8,128)} %vel_hbm.1, f32[9,64,128]{2,1,0:T(8,128)} %aff_hbm.1, ...), custom_call_target="tpu_custom_call" | custom-call | tf_op jit(solution)/shard_map/pallas_call | solution.py:691
  44.3 2.3 %shard_map.114 = (f32[24,64,128]{2,1,0:T(8,128)}, f32[25,64,128]{2,1,0:T(8,128)}) custom-call(f32[24,64,128]{2,1,0:T(8,128)} %get-tuple-element.4.state, f32[25,64,128]{2,1,0:T(8,128)} %get-tuple-element.5.arrivals), custom_call_target="tpu_custom_call" | custom-call | tf_op jit(solution)/shard_map/pallas_call | solution.py:754

commit v5 on v4

--- a/solution.py
+++ b/solution.py
@@ -23,9 +23,10 @@
 gravity = (2.0, 0.0, -9.0)
 mass_floor = 1.0
 move_list = ((-1, -1), (-1, 0), (-1, 1), (0, -1), (0, 1), (1, -1), (1, 0), (1, 1))
-early_order = (0, 2, 5, 7, 3, 4, 1, 6)
+early_order = (0, 2, 1, 6, 5, 7, 3, 4)
 arrival_order = (1, 6, 0, 2, 5, 7, 3, 4)
-early_first = 4
+early_first = 6
+late_order = (0, 2, 5, 7, 3, 4, 1, 6)
 p2g_batch = 8
 g2p_batch = 8
 
@@ -537,7 +538,7 @@
         q = lax.rem(column, NBY)
         return [node_v[2 * p + x, q + yp] for x in range(4) for yp in range(2)]
 
-    for move in early_order:
+    for move in late_order:
         packed = [jnp.zeros((8, 128), f32)] * 4
         for k in range(8):
             b = source_of(move * 8 + k)
@@ -658,7 +659,7 @@
 
 
 def pass_on(state, arrivals, state_out, arrive_out, held, held_too, in_sem, out_sem):
-    chunks = [(state, held, state_out, pl.ds(6 * n, 6)) for n in range(4)]
+    chunks = [(state, held, state_out, pl.ds(12 * n, 12)) for n in range(2)]
     chunks += [(arrivals, held_too, arrive_out, pl.ds(5 * n, 5)) for n in range(5)]
     taken = [pltpu.make_async_copy(a.at[d], v.at[d], in_sem.at[n]) for n, (a, v, _, d) in enumerate(chunks)]
     given = [pltpu.make_async_copy(v.at[d], o.at[d], out_sem.at[n]) for n, (_, v, o, d) in enumerate(chunks)]
@@ -762,8 +763,8 @@
         scratch_shapes=[
             pltpu.VMEM((24, BLOCKS, SLOTS), f32),
             pltpu.VMEM((25, BLOCKS, SLOTS), f32),
-            dma((9,)),
-            dma((9,)),
+            dma((7,)),
+            dma((7,)),
         ],
     )(*results)
 

time: 46.8 us -> 46.6 us (level)
  Pallas kernels: 46 us -> 45.4 us
    pallas_call x1, Pallas kernels: 43.7 us -> 43.1 us  [body(): pl.pallas_call(functools.partial(kernel, n_down, n_cross), out_shape=(jax...]
where the time goes in v5:
time: 46.6 us; the launch traced here: 46 us
  Pallas kernels  45.4 us (97%)
  between operations  0.64 us (1%)
    pallas_call x1, Pallas kernels, body(): pl.pallas_call(functools.partial(kernel, n_down, n_cross), out_shape=(jax...  43.1 us
    pallas_call x1, Pallas kernels, body(): pl.pallas_call(pass_on, out_shape=(jax.ShapeDtypeStruct((24, BLOCKS, SLOT...  2.26 us

profile of v5, /device:TPU:28, one launch (start us, length us, event | category | flops | bytes accessed | tf_op | source)
XLA Modules:
  0.0 46.0 jit_solution(6514447243304129269)
XLA Ops:
  0.6 43.1 %shard_map.113 = (f32[24,64,128]{2,1,0:T(8,128)}, f32[25,64,128]{2,1,0:T(8,128)}) custom-call(s32[1,64]{1,0:T(1,128)} %bitcast.6, s32[1,64]{1,0:T(1,128)} %bitcast.7, s32[1,64]{1,0:T(1,128)} %bitcast.8, s32[1,64]{1,0:T(1,128)} %bitcast.9, f32[3,64,128]{2,1,0:T(8,128)} %pos_hbm.1, f32[3,64,128]{2,1,0:T(8,128)} %vel_hbm.1, f32[9,64,128]{2,1,0:T(8,128)} %aff_hbm.1, ...), custom_call_target="tpu_custom_call" | custom-call | tf_op jit(solution)/shard_map/pallas_call | solution.py:692
  43.7 2.3 %shard_map.114 = (f32[24,64,128]{2,1,0:T(8,128)}, f32[25,64,128]{2,1,0:T(8,128)}) custom-call(f32[24,64,128]{2,1,0:T(8,128)} %get-tuple-element.4.state, f32[25,64,128]{2,1,0:T(8,128)} %get-tuple-element.5.arrivals), custom_call_target="tpu_custom_call" | custom-call | tf_op jit(solution)/shard_map/pallas_call | solution.py:755
